TPU v7x, 16 devices: a whole 2x2x2 slice. The times are simulated.
16 devices in a mesh: fsdp: 16 (over z, y, x, core).
Axes of the slice: x: 2, y: 2, z: 2, core: 2. Of those that a mesh axis runs over, the one named last changes fastest.
Arguments:
- token_ids: int32 [16, 512], P('fsdp')
- grad_y: bfloat16 [16, 512, 1536], P('fsdp')
- table: bfloat16 [151936, 1536], P('fsdp')
- norm1_gain: bfloat16 [1536], P('fsdp')
- norm2_gain: bfloat16 [1536], P('fsdp')
- w_query: bfloat16 [1536, 12, 128], P('fsdp')
- w_key: bfloat16 [1536, 2, 128], P('fsdp')
- w_value: bfloat16 [1536, 2, 128], P('fsdp')
- w_out: bfloat16 [1536, 1536], P('fsdp')
- w_gate: bfloat16 [1536, 8960], P('fsdp')
- w_up: bfloat16 [1536, 8960], P('fsdp')
- w_down: bfloat16 [8960, 1536], P('fsdp')
Outputs:
- output 1: bfloat16 [16, 512, 1536], P('fsdp')
- output 2: bfloat16 [151936, 1536], P('fsdp')
- output 3: bfloat16 [1536], P('fsdp')
- output 4: bfloat16 [1536], P('fsdp')
- output 5: bfloat16 [1536, 12, 128], P('fsdp')
- output 6: bfloat16 [1536, 2, 128], P('fsdp')
- output 7: bfloat16 [1536, 2, 128], P('fsdp')
- output 8: bfloat16 [1536, 1536], P('fsdp')
- output 9: bfloat16 [1536, 8960], P('fsdp')
- output 10: bfloat16 [1536, 8960], P('fsdp')
- output 11: bfloat16 [8960, 1536], P('fsdp')
All inputs are finite; a program needn't handle non-finite values.
Results may differ from a plain program's by a relative error of at most 0.0153617.
Values are sent between devices in bfloat16 or wider.
A program may use at most 1 GiB of HBM per device.

v0:
```python
import jax
import jax.numpy as jnp
import numpy as np
from jax import lax
from jax.experimental import pallas as pl
from jax.experimental.pallas import tpu as pltpu
from jax.sharding import PartitionSpec as P


ALL = ("z", "y", "x", "c")
PLANE = ("z", "y")
N_DEV = 16
NORM_EPS = 1e-5
ROPE_THETA = 500000.0
SLOTS = 48
USABLE = SLOTS - 2
ROW_BLOCK = 512
CHUNKS = 2
F32 = jnp.float32
BF16 = jnp.bfloat16
MESH = pl.DeviceIdType.MESH


def rms_norm(x_f32, gain_f32):
    inv_rms = lax.rsqrt(jnp.mean(x_f32 * x_f32, axis=-1, keepdims=True) + NORM_EPS)
    return (x_f32 * inv_rms * gain_f32).astype(BF16)


def rotary(x_f32):
    head_dim = x_f32.shape[-1]
    half_dim = head_dim // 2
    seq_len = x_f32.shape[-3]
    inv_freq = np.float32(ROPE_THETA) ** (np.float32(-2.0) * np.arange(half_dim, dtype=np.float32) / np.float32(head_dim))
    angles = (np.arange(seq_len, dtype=np.float32)[:, None] * inv_freq[None, :]).astype(np.float32)
    cos_tab = jnp.asarray(np.cos(angles))[:, None, :]
    sin_tab = jnp.asarray(np.sin(angles))[:, None, :]
    lo_half = x_f32[..., :half_dim]
    hi_half = x_f32[..., half_dim:]
    return jnp.concatenate([lo_half * cos_tab - hi_half * sin_tab, hi_half * cos_tab + lo_half * sin_tab], axis=-1)


def attend(q_f32, k_f32, v_bf16):
    batch_loc, seq_len, q_heads, head_dim = q_f32.shape
    kv_heads = k_f32.shape[2]
    q_rot = rotary(q_f32).astype(BF16).reshape(batch_loc, seq_len, kv_heads, q_heads // kv_heads, head_dim)
    k_rot = rotary(k_f32).astype(BF16)
    scores = jnp.einsum("bqkgd,bskd->bkgqs", q_rot, k_rot, preferred_element_type=F32) * head_dim ** -0.5
    positions = jnp.arange(seq_len)
    causal = positions[:, None] >= positions[None, :]
    scores = jnp.where(causal, scores, -1e30)
    prob_bf = jax.nn.softmax(scores, axis=-1).astype(BF16)
    attn_out = jnp.einsum("bkgqs,bskd->bqkgd", prob_bf, v_bf16, preferred_element_type=F32)
    return attn_out.astype(BF16).reshape(batch_loc, seq_len, q_heads * head_dim)


def gated(gate_f32, up_f32):
    return (jax.nn.silu(gate_f32) * up_f32).astype(BF16)


def dot(a, b, ca, cb):
    return lax.dot_general(a, b, (((ca,), (cb,)), ((), ())), preferred_element_type=F32)


def flip(a, axis):
    return lax.ppermute(a, axis, [(0, 1), (1, 0)])


def pick_dim(a, index, dim):
    return lax.dynamic_index_in_dim(a, index, dim, keepdims=False)


def row_sum_kernel(start_ref, slot_ref, row_ref, recv_ref, out_ref, acc):
    blk = pl.program_id(0)
    acc[...] = jnp.zeros_like(acc)

    def add_row(i, carry):
        r = row_ref[i] - blk * ROW_BLOCK
        acc[pl.ds(r, 1), :] += recv_ref[pl.ds(slot_ref[i], 1), :]
        return carry

    lax.fori_loop(start_ref[blk], start_ref[blk + 1], add_row, 0)
    out_ref[...] = acc[...].astype(BF16)


def row_sums(starts, slots, rows, recv, rows_dev):
    width = recv.shape[1]
    n_blk = pl.cdiv(rows_dev, ROW_BLOCK)
    return pl.pallas_call(
        row_sum_kernel,
        out_shape=jax.ShapeDtypeStruct((rows_dev, width), BF16),
        grid_spec=pltpu.PrefetchScalarGridSpec(
            num_scalar_prefetch=3,
            grid=(n_blk,),
            in_specs=[pl.BlockSpec(recv.shape, lambda i, *_: (0, 0))],
            out_specs=pl.BlockSpec((ROW_BLOCK, width), lambda i, *_: (i, 0)),
            scratch_shapes=[pltpu.VMEM((ROW_BLOCK, width), F32)],
        ),
        cost_estimate=pl.CostEstimate(flops=40_000_000_000, bytes_accessed=40_000_000, transcendentals=0),
    )(starts, slots, rows, recv)


def flipped(mask):
    here = [lax.axis_index(n) for n in ALL]
    return tuple(1 - v if (mask >> (3 - i)) & 1 else v for i, v in enumerate(here))


def enter_all():
    barrier = pltpu.get_barrier_semaphore()
    for m in range(1, N_DEV):
        pl.semaphore_signal(barrier, inc=1, device_id=flipped(m), device_id_type=MESH)
    pl.semaphore_wait(barrier, N_DEV - 1)


def share_kernel(in_ref, out_ref, send_sem, recv_sem):
    me = lax.axis_index(ALL)
    enter_all()
    copies = []
    for m in range(1, N_DEV):
        copies.append(
            pltpu.make_async_remote_copy(
                src_ref=in_ref, dst_ref=out_ref.at[me], send_sem=send_sem.at[m], recv_sem=recv_sem.at[m], device_id=flipped(m), device_id_type=MESH
            )
        )
        copies[-1].start()
    out_ref[me] = in_ref[...]
    for copy in copies:
        copy.wait()


def exchange(kernel, array, out_shape, collective_id, flops):
    return pl.pallas_call(
        kernel,
        out_shape=jax.ShapeDtypeStruct(out_shape, array.dtype),
        in_specs=[pl.BlockSpec(memory_space=pltpu.VMEM)],
        out_specs=pl.BlockSpec(memory_space=pltpu.VMEM),
        scratch_shapes=[pltpu.SemaphoreType.DMA((N_DEV,)), pltpu.SemaphoreType.DMA((N_DEV,))],
        compiler_params=pltpu.CompilerParams(collective_id=collective_id, has_side_effects=True),
        cost_estimate=pl.CostEstimate(flops=flops, bytes_accessed=2 * array.size, transcendentals=0),
    )(array)


def pair_kernel(own_ref, far_ref, out_ref, local_sem, send_sem, recv_sem):
    x_i, c_i = lax.axis_index("x"), lax.axis_index("c")
    other = flipped(1)
    barrier = pltpu.get_barrier_semaphore()
    pl.semaphore_signal(barrier, inc=1, device_id=other, device_id_type=MESH)
    pl.semaphore_wait(barrier, 1)
    copies = []
    for k, (ref, px) in enumerate(((own_ref, x_i), (far_ref, 1 - x_i))):
        to = out_ref.at[:, px, c_i]
        copies.append(
            pltpu.make_async_remote_copy(src_ref=ref, dst_ref=to, send_sem=send_sem.at[k], recv_sem=recv_sem.at[k], device_id=other, device_id_type=MESH)
        )
        copies.append(pltpu.make_async_copy(ref, to, local_sem.at[k]))
    for copy in copies:
        copy.start()
    for copy in copies:
        copy.wait()


def gather_xc(w, collective_id):
    far = flip(w, "x")
    a, r, n = w.shape
    return pl.pallas_call(
        pair_kernel,
        out_shape=jax.ShapeDtypeStruct((a, 2, 2, r, n), w.dtype),
        in_specs=[pl.BlockSpec(memory_space=pltpu.VMEM)] * 2,
        out_specs=pl.BlockSpec(memory_space=pl.ANY),
        scratch_shapes=[pltpu.SemaphoreType.DMA((2,))] * 3,
        compiler_params=pltpu.CompilerParams(collective_id=collective_id, has_side_effects=True),
        cost_estimate=pl.CostEstimate(flops=60_000_000, bytes_accessed=8 * w.size, transcendentals=0),
    )(w, far)


def solution(mesh):
    mesh = jax.sharding.Mesh(mesh.devices.reshape(2, 2, 2, 2), ALL)
    spec_1d = P(ALL)
    spec_2d = P(ALL, None)
    spec_3d = P(ALL, None, None)
    in_specs = (spec_2d, spec_3d, spec_2d, spec_1d, spec_1d, spec_3d, spec_3d, spec_3d, spec_2d, spec_2d, spec_2d, spec_2d)
    out_specs = (spec_3d, spec_2d, spec_1d, spec_1d, spec_3d, spec_3d, spec_3d, spec_2d, spec_2d, spec_2d, spec_2d)

    def step(token_ids, grad_y, table, gain1, gain2, w_query, w_key, w_value, w_out, w_gate, w_up, w_down):
        seq = token_ids.shape[1]
        rows_dev, dim = table.shape
        shard = w_gate.shape[0]
        ffn = w_gate.shape[1]
        ffn_q = ffn // 4
        q_w = w_query.shape[1] * w_query.shape[2]
        kv_w = w_key.shape[1] * w_key.shape[2]
        step_t = seq // CHUNKS
        me = lax.axis_index(ALL)
        z_i, y_i, x_i, c_i = (lax.axis_index(n) for n in ALL)

        small = jnp.concatenate([token_ids[0].astype(F32), gain1.astype(F32), gain2.astype(F32), jnp.zeros((1024 - seq - 2 * shard,), F32)])
        small = exchange(share_kernel, small.reshape(8, 128), (N_DEV, 8, 128), 0, 20_000_000)
        small = small.reshape(N_DEV, 1024)
        ids_all = small[:, :seq].astype(jnp.int32)
        g1_full = small[:, seq : seq + shard].reshape(-1)
        g2_full = small[:, seq + shard : seq + 2 * shard].reshape(-1)

        owner = ids_all // rows_dev
        pos = jnp.arange(seq)
        before = pos[None, :] < pos[:, None]
        same = ids_all[:, :, None] == ids_all[:, None, :]
        first = jnp.logical_not(jnp.any(same & before[None], axis=2))
        mine = first & (owner == me)
        owner_is = (owner[:, :, None] == jnp.arange(N_DEV)) & first[:, :, None]
        overflow = jnp.max(jnp.sum(owner_is.astype(jnp.int32), axis=1)) > USABLE
        rank = dot(mine.astype(BF16), before.astype(BF16), 1, 1).astype(jnp.int32)
        in_slot = mine[:, None, :] & (rank[:, None, :] == jnp.arange(SLOTS)[None, :, None])
        rel = ids_all - me * rows_dev
        slot_row = jnp.sum(jnp.where(in_slot, rel[:, None, :], 0), axis=2)
        slot_used = jnp.any(in_slot, axis=2)
        spread = (jnp.arange(N_DEV * SLOTS).reshape(N_DEV, SLOTS) * 12) % rows_dev
        fetch_row = jnp.where(slot_used, slot_row, spread)
        ids_me = token_ids[0]
        own_me = ids_me // rows_dev
        same_me = ids_me[:, None] == ids_me[None, :]
        first_me = jnp.logical_not(jnp.any(same_me & before, axis=1))
        rank_me = jnp.sum(((own_me[:, None] == own_me[None, :]) & before & first_me[None, :]).astype(jnp.int32), axis=1)
        slot_first = own_me * SLOTS + rank_me
        slot_tok = jnp.sum(jnp.where(same_me & first_me[None, :], slot_first[None, :], 0), axis=1)
        pick = (slot_tok[:, None] == jnp.arange(N_DEV * SLOTS)[None, :]).astype(BF16)

        sent = table.at[fetch_row.reshape(-1)].get(mode="promise_in_bounds").reshape(N_DEV, SLOTS, dim)
        got = lax.all_to_all(sent, ALL, 0, 0, tiled=True)
        emb_fast = dot(pick, got.reshape(-1, dim), 1, 0).astype(BF16)

        def ring(k):
            return [(d, (d + k) % N_DEV) for d in range(N_DEV)]

        def emb_dense():
            owned = owner == me
            picked = jnp.take(table, jnp.where(owned, rel, 0), axis=0)
            part = jnp.where(owned[:, :, None], picked, jnp.zeros((), BF16))
            total = pick_dim(part, me, 0)
            for k in range(1, N_DEV):
                total += lax.ppermute(pick_dim(part, (me + k) % N_DEV, 0), ALL, ring(k))
            return total

        emb = lax.cond(overflow, emb_dense, lambda: emb_fast)

        w_qkv = jnp.concatenate([w_query.reshape(shard, -1), w_key.reshape(shard, -1), w_value.reshape(shard, -1)], axis=1)
        w_qkv = lax.all_gather(w_qkv, ALL, axis=0, tiled=True)
        w_o = lax.all_gather(w_out, ALL, axis=0, tiled=True)
        dy = grad_y[0]
        dy_z, dy_y = flip(dy, "z"), flip(dy, "y")
        dy_far = jnp.concatenate([flip(dy_z[:, : dim // 2], "y"), flip(dy_y[:, dim // 2 :], "z")], axis=1)
        dys = lax.dynamic_update_slice(jnp.zeros((CHUNKS, 2, 2, step_t, dim), BF16), dy.reshape(CHUNKS, 1, 1, step_t, dim), (0, z_i, y_i, 0, 0))
        for block, at_z, at_y in ((dy_z, 1 - z_i, y_i), (dy_y, z_i, 1 - y_i), (dy_far, 1 - z_i, 1 - y_i)):
            dys = lax.dynamic_update_slice(dys, block.reshape(CHUNKS, 1, 1, step_t, dim), (0, at_z, at_y, 0, 0))
        dys = dys.reshape(CHUNKS, 4 * step_t, dim)

        def wide(w, collective_id):
            cols = jnp.stack([w[:, k * ffn_q : (k + 1) * ffn_q] for k in range(4)])
            cols = lax.all_to_all(cols, PLANE, 0, 0, tiled=True)
            return gather_xc(cols, collective_id).reshape(dim, ffn_q)

        w_d = gather_xc(w_down[None], 2).reshape(ffn_q, dim)
        w_g = wide(w_gate, 3)
        w_u = wide(w_up, 4)

        x_f32 = emb.astype(F32)
        h_one, norm1_pull = jax.vjp(rms_norm, x_f32, g1_full)
        qkv = dot(h_one, w_qkv, 1, 0)
        q_f32 = qkv[:, :q_w].reshape(1, seq, -1, 128)
        k_f32 = qkv[:, q_w : q_w + kv_w].reshape(1, seq, -1, 128)
        v_bf16 = qkv[:, q_w + kv_w :].astype(BF16).reshape(1, seq, -1, 128)
        attn_out, attn_pull = jax.vjp(attend, q_f32, k_f32, v_bf16)
        o_bf = attn_out[0]
        resid_bf = (x_f32 + dot(o_bf, w_o, 1, 0)).astype(BF16)
        resid_two = resid_bf.astype(F32)
        h_two, norm2_pull = jax.vjp(rms_norm, resid_two, g2_full)

        def add_flip(part, index, dim_at, axis, cols=slice(None)):
            keep, give = pick_dim(part, index, dim_at)[..., cols], pick_dim(part, 1 - index, dim_at)[..., cols]
            got_half = flip(give, axis)
            return keep + got_half

        def plane_sum(part):
            part = lax.optimization_barrier(part).reshape(2, 2, -1, dim)
            a = add_flip(part, z_i, 0, "z", slice(dim // 2))
            b = add_flip(part, y_i, 1, "y", slice(dim // 2, dim))
            return jnp.concatenate([add_flip(a, y_i, 0, "y"), add_flip(b, z_i, 0, "z")], axis=1)

        hs, acts, d_gates, d_ups, d_hs, y_sums = [], [], [], [], [], []
        for k in range(CHUNKS):
            h_k = lax.all_gather(h_two[k * step_t : (k + 1) * step_t], PLANE, axis=0, tiled=True)
            d_act = dot(dys[k], w_d, 1, 1).astype(BF16)
            up_f32 = dot(h_k, w_u, 1, 0)
            gate_f32 = dot(h_k, w_g, 1, 0)
            act_k, act_pull = jax.vjp(gated, gate_f32, up_f32)
            d_gate, d_up = act_pull(d_act)
            act_k, d_gate, d_up = lax.optimization_barrier((act_k, d_gate.astype(BF16), d_up.astype(BF16)))
            d_h_part = dot(d_gate, w_g, 1, 1) + dot(d_up, w_u, 1, 1)
            d_hs.append(lax.psum_scatter(d_h_part, PLANE, scatter_dimension=0, tiled=True).astype(BF16))
            y_part = dot(act_k, w_d, 1, 0)
            y_sums.append(plane_sum(y_part))
            hs.append(h_k)
            acts.append(act_k)
            d_gates.append(d_gate)
            d_ups.append(d_up)
        d_h_two = jnp.concatenate(d_hs)
        y_sum, resid_y = lax.optimization_barrier((jnp.concatenate(y_sums), resid_bf))
        layer_out = (resid_y.astype(F32) + y_sum).astype(BF16)
        h_all, d_gate, d_up = (jnp.concatenate(v) for v in (hs, d_gates, d_ups))
        act, dy_all = jnp.concatenate(acts), dys.reshape(-1, dim)

        def grad_xc(a, b, shape, c_dim):
            part = dot(a, b, 0, 0).reshape(shape)
            half = add_flip(part, c_i, c_dim, "c")
            return add_flip(half, x_i, c_dim - 1, "x").astype(BF16)

        def grad_all(a, b):
            part = dot(a, b, 0, 0).reshape(4, 2, 2, shard, -1)
            half = add_flip(part, c_i, 2, "c")
            half = lax.psum_scatter(half.reshape(8 * shard, -1), PLANE, scatter_dimension=0, tiled=True)
            return add_flip(half.reshape(2, shard, -1), x_i, 0, "x").astype(BF16)

        cols = (4, 2, 2, shard, ffn_q)
        g_gate = grad_xc(h_all, d_gate, cols, 2)
        g_up = grad_xc(h_all, d_up, cols, 2)
        g_down = grad_xc(act, dy_all, (2, 2, ffn // N_DEV, dim), 1)
        back = lax.all_to_all(jnp.stack([g_gate, g_up], axis=1), PLANE, 0, 0, tiled=True)
        back = back.transpose(1, 2, 0, 3).reshape(2, shard, ffn)

        d_resid_two, g_norm2 = norm2_pull(d_h_two)
        d_resid = (dy.astype(F32) + d_resid_two).astype(BF16)
        g_out = grad_all(o_bf, d_resid)
        d_attn = dot(d_resid, w_o, 1, 1).astype(BF16)
        d_query, d_key, d_value = attn_pull(d_attn[None])
        d_qkv = jnp.concatenate([d_query.astype(BF16).reshape(seq, -1), d_key.astype(BF16).reshape(seq, -1), d_value.reshape(seq, -1)], axis=1)
        g_qkv = grad_all(h_one, d_qkv)
        d_h_one = dot(d_qkv, w_qkv, 1, 1).astype(BF16)
        d_x, g_norm1 = norm1_pull(d_h_one)
        d_emb = (d_resid.astype(F32) + d_x).astype(BF16)

        d_slot = dot(pick, d_emb, 0, 0).reshape(N_DEV, SLOTS, dim)
        place = jnp.arange(SLOTS)[None, :, None]
        d_slot = jnp.where(place == USABLE, g_norm1, jnp.where(place == USABLE + 1, g_norm2, d_slot))
        d_got = lax.all_to_all(d_slot, ALL, 0, 0, tiled=True)
        gains = lax.dynamic_slice_in_dim(jnp.sum(d_got[:, USABLE:], axis=0), me * shard, shard, axis=1).astype(BF16)
        n_slot = N_DEV * SLOTS
        key = jnp.where(slot_used, slot_row, rows_dev).reshape(-1)
        key_sorted, order = lax.sort((key, jnp.arange(n_slot, dtype=jnp.int32)), num_keys=1)
        edges = jnp.minimum(jnp.arange(pl.cdiv(rows_dev, ROW_BLOCK) + 1) * ROW_BLOCK, rows_dev)
        starts = jnp.sum((key[None, :] < edges[:, None]).astype(jnp.int32), axis=1)

        def rows_dense():
            d_all = jnp.concatenate([d_emb] + [lax.ppermute(d_emb, ALL, ring(k)) for k in range(1, N_DEV)])
            origin = (me - jnp.arange(N_DEV)) % N_DEV
            seg = jnp.where(owner == me, rel, rows_dev)[origin].reshape(-1)
            return jax.ops.segment_sum(d_all.astype(F32), seg, num_segments=rows_dev).astype(BF16)

        d_rows = lax.cond(overflow, rows_dense, lambda: row_sums(starts, order, key_sorted, d_got.reshape(-1, dim), rows_dev))
        g_q = g_qkv[:, :q_w].reshape(w_query.shape)
        g_k = g_qkv[:, q_w : q_w + kv_w].reshape(w_key.shape)
        g_v = g_qkv[:, q_w + kv_w :].reshape(w_value.shape)
        return layer_out[None], d_rows, gains[0], gains[1], g_q, g_k, g_v, g_out, back[0], back[1], g_down

    return jax.shard_map(step, mesh=mesh, in_specs=in_specs, out_specs=out_specs, check_vma=False)
```

profile of v0, /device:TPU:0, one launch (start us, length us, event | category | flops | bytes accessed | tf_op | source)
XLA Modules:
  0.0 988.2 jit_solution(13928740403585305332)
XLA Ops:
  12.6 9.2 shard_map.239
  22.8 4.2 and_reduce_fusion
  28.4 18.9 %gather_fusion.2 = bf16[768,1536]{1,0:T(8,128)(2,1)} fusion(bf16[9496,1536]{1,0:T(8,128)(2,1)} %param.22, s32[1024]{0:T(1024)S(1)} %pad_clamp_fusion.1), kind=kCustom, calls=%fused_computation.2 | custom fusion | bytes 4721664 | tf_op jit(solution)/shard_map/gather | solution.py:226
  54.4 29.2 %all-to-all-done = bf16[16,48,1536]{2,1,0:T(8,128)(2,1)S(1)} async-done(((bf16[16,48,1536]{2,1,0:T(8,128)(2,1)}), bf16[16,48,1536]{2,1,0:T(8,128)(2,1)S(1)}, u32[]{:S(2)}, u32[]{:S(2)}) %all-to-all-start) | async-done | bytes 2359328 | tf_op jit(solution)/shard_map/all_to_all | solution.py:227
  85.0 5.4 conditional.2
  96.9 4.8 all-to-all-start.2
  105.4 5.6 fusion.145
  137.4 6.0 fusion.80
  143.4 5.7 fusion.72
  173.8 16.3 %all-to-all-done.1.own_ref = bf16[4,96,2240]{2,1,0:T(8,128)(2,1)S(1)} async-done(((bf16[4,96,2240]{2,1,0:T(8,128)(2,1)}), bf16[4,96,2240]{2,1,0:T(8,128)(2,1)S(1)}, u32[]{:S(2)}, u32[]{:S(2)}) %all-to-all-start.1) | async-done | bytes 1720352 | tf_op jit(solution)/shard_map/all_to_all | solution.py:257
  196.5 8.2 shard_map.242
  204.8 4.2 collective-permute-done.35
  212.7 5.7 fusion.146
  218.4 8.9 convolution_convert_fusion
  227.3 22.6 %collective-permute-done.30.far_ref = bf16[4,96,2240]{2,1,0:T(8,128)(2,1)} collective-permute-done((bf16[4,96,2240]{2,1,0:T(8,128)(2,1)S(1)}, bf16[4,96,2240]{2,1,0:T(8,128)(2,1)}, u32[]{:S(2)}, u32[]{:S(2)}) %collective-permute-start.30) | collective-permute-done | bytes 1720352 | tf_op jit(solution)/shard_map/ppermute | solution.py:65
  249.9 8.4 shard_map.240
  258.3 8.4 shard_map.241
  266.8 13.8 %fusion.154 = f32[1024,2240]{0,1:T(8,128)} fusion(bf16[1024,1536]{1,0:T(8,128)(2,1)} %all-gather.11.cloned.1.call-done, bf16[1536,2240]{1,0:T(8,128)(2,1)} %bitcast.479), kind=kOutput, calls=%fused_computation.344 | convolution fusion | flops 7046430720 | bytes 19202048 | tf_op jit(solution)/shard_map/dot_general | solution.py:61
  280.6 20.3 %fusion.38 = (bf16[1024,2240]{0,1:T(8,128)(2,1)}, bf16[1024,2240]{0,1:T(8,128)(2,1)}, bf16[1024,2240]{0,1:T(8,128)(2,1)}) fusion(f32[1024,2240]{0,1:T(8,128)} %fusion.154, bf16[1024,2240]{0,1:T(8,128)(2,1)} %convolution_convert_fusion, bf16[1024,1536]{1,0:T(8,128)(2,1)S(1)} %copy-done.39, bf16[1536,2240]{1,0:T(8,128)(2,1)} %bitcast.475), kind=kOutput, calls=%fused_computation.99 | convolution fusion | flops 7085424640 | bytes 37552128 | tf_op jit(solution)/shard_map/dot_general | solution.py:61
  300.9 11.9 %fusion.157 = f32[1024,1536]{1,0:T(8,128)S(1)} fusion(bf16[1024,2240]{0,1:T(8,128)(2,1)} %get-tuple-element.83, bf16[1536,2240]{1,0:T(8,128)(2,1)} %bitcast.480), kind=kOutput, calls=%fused_computation.347 | convolution fusion | flops 7046430720 | bytes 17760256 | tf_op jit(solution)/shard_map/dot_general | solution.py:61
  312.8 11.8 %convolution_add_fusion = f32[1024,1536]{1,0:T(8,128)} fusion(f32[1024,1536]{1,0:T(8,128)S(1)} %fusion.157, bf16[1024,2240]{0,1:T(8,128)(2,1)S(1)} %copy-done.101, bf16[1536,2240]{1,0:T(8,128)(2,1)} %bitcast.476), kind=kOutput, calls=%fused_computation.138 | convolution fusion | flops 7048003584 | bytes 24051712 | tf_op jit(solution)/shard_map/dot_general | solution.py:61
  324.6 11.9 %convolution_convert_fusion.1 = bf16[1024,2240]{0,1:T(8,128)(2,1)} fusion(bf16[1024,1536]{1,0:T(8,128)(2,1)} %bitcast.503, bf16[2240,1536]{1,0:T(8,128)(2,1)} %bitcast.483), kind=kOutput, calls=%fused_computation.128 | convolution fusion | flops 7048724480 | bytes 14614528 | tf_op jit(solution)/shard_map/dot_general | solution.py:61
  336.6 13.2 %fusion.152 = f32[1024,2240]{0,1:T(8,128)} fusion(bf16[1024,1536]{1,0:T(8,128)(2,1)} %all-gather.9.cloned.1.call-done, bf16[1536,2240]{1,0:T(8,128)(2,1)} %bitcast.481), kind=kOutput, calls=%fused_computation.342 | convolution fusion | flops 7046430720 | bytes 19202048 | tf_op jit(solution)/shard_map/dot_general | solution.py:61
  349.8 22.4 %fusion.35 = (bf16[1024,2240]{0,1:T(8,128)(2,1)}, bf16[1024,2240]{0,1:T(8,128)(2,1)}, bf16[1024,2240]{0,1:T(8,128)(2,1)}) fusion(f32[1024,2240]{0,1:T(8,128)} %fusion.152, bf16[1024,2240]{0,1:T(8,128)(2,1)} %convolution_convert_fusion.1, bf16[1024,1536]{1,0:T(8,128)(2,1)} %all-gather.9.cloned.1.call-done, bf16[1536,2240]{1,0:T(8,128)(2,1)} %bitcast.477), kind=kOutput, calls=%fused_computation.96 | convolution fusion | flops 7085424640 | bytes 37552128 | tf_op jit(solution)/shard_map/dot_general | solution.py:61
  372.1 11.4 %fusion.156 = f32[1024,1536]{1,0:T(8,128)S(1)} fusion(bf16[1024,2240]{0,1:T(8,128)(2,1)} %get-tuple-element.81, bf16[1536,2240]{1,0:T(8,128)(2,1)} %bitcast.482), kind=kOutput, calls=%fused_computation.346 | convolution fusion | flops 7046430720 | bytes 17760256 | tf_op jit(solution)/shard_map/dot_general | solution.py:61
  383.5 11.9 %convolution_add_fusion.1 = f32[1024,1536]{1,0:T(8,128)} fusion(f32[1024,1536]{1,0:T(8,128)S(1)} %fusion.156, bf16[1024,2240]{0,1:T(8,128)(2,1)S(1)} %copy-done.102, bf16[1536,2240]{1,0:T(8,128)(2,1)} %bitcast.478), kind=kOutput, calls=%fused_computation.139 | convolution fusion | flops 7048003584 | bytes 24051712 | tf_op jit(solution)/shard_map/dot_general | solution.py:61
  396.2 4.4 sort.15
  401.9 11.5 %fusion.155 = f32[1024,1536]{1,0:T(8,128)S(1)} fusion(bf16[1024,2240]{0,1:T(8,128)(2,1)} %get-tuple-element.77, bf16[2240,1536]{1,0:T(8,128)(2,1)} %bitcast.484), kind=kOutput, calls=%fused_computation.345 | convolution fusion | flops 7046430720 | bytes 17760256 | tf_op jit(solution)/shard_map/dot_general | solution.py:61
  422.1 20.0 %fusion.43 = f32[1536,2240]{1,0:T(8,128)S(1)} fusion(bf16[2048,1536]{1,0:T(8,128)(2,1)S(1)} %constant_dynamic-update-slice_fusion.20, bf16[1024,2240]{0,1:T(8,128)(2,1)} %get-tuple-element.83, bf16[1024,2240]{0,1:T(8,128)(2,1)} %get-tuple-element.81), kind=kOutput, calls=%fused_computation.104 | convolution fusion | flops 14111211520 | bytes 29229056 | tf_op jit(solution)/shard_map/dot_general | solution.py:61
  442.2 3.8 dynamic-slice_bitcast_fusion.15
  446.1 5.9 copy-done.11
  452.3 21.1 %fusion.39 = f32[1536,2240]{1,0:T(8,128)S(1)} fusion(bf16[2048,1536]{1,0:T(8,128)(2,1)} %copy-done.41, bf16[1024,2240]{0,1:T(8,128)(2,1)} %get-tuple-element.82, bf16[1024,2240]{0,1:T(8,128)(2,1)} %get-tuple-element.80), kind=kOutput, calls=%fused_computation.100 | convolution fusion | flops 14111211520 | bytes 29229056 | tf_op jit(solution)/shard_map/dot_general | solution.py:61
  473.4 3.7 dynamic-slice_bitcast_fusion.16
  480.8 4.0 pad_maximum_fusion
  493.1 5.0 convolution_convert_fusion.4
  498.9 8.1 fusion.29
  507.1 11.2 %fusion.109 = f32[1,512,2,128]{3,1,2,0:T(8,128)S(1)} fusion(bf16[2,6,512,512]{2,3,1,0:T(8,128)(2,1)S(1)} %get-tuple-element.231, f32[2,6,512]{2,1,0:T(8,128)S(1)} %neg.22, f32[2,6,512]{2,1,0:T(8,128)S(1)} %copy-done.75, pred[512,512]{0,1:T(8,128)(4,1)S(1)} %copy-done.38, f32[2,512,512,6]{2,1,3,0:T(8,128)} %copy-done.2, f32[2,6,512]{2,1,0:T(8,128)S(1)} %copy-done.71, ...), kind=kOutput, calls=%fused_computation.224 | convolution fusion | flops 837025792 | bytes 21307392 | tf_op jit(solution)/shard_map/transpose(jvp(bqkgd,bskd->bkgqs))/dot_general | solution.py:47
  519.7 4.6 fusion.84
  528.4 9.3 bitcast_convert_fusion
  541.6 5.9 fusion.97
  547.5 5.2 fusion.113
  559.1 5.4 bitcast_add_fusion.5
  564.6 18.8 %fusion.158 = f32[2,2,560,1536]{3,2,1,0:T(8,128)S(1)} fusion(bf16[2,2,560,2048]{3,2,1,0:T(8,128)(2,1)} %bitcast.474, bf16[2048,1536,1,1]{1,0,3,2:T(8,128)(2,1)} %bitcast.149), kind=kOutput, calls=%fused_computation.348 | convolution fusion | flops 14092861440 | bytes 29229056 | tf_op jit(solution)/shard_map/dot_general | solution.py:61
  583.4 3.8 dynamic-slice_bitcast_fusion.17
  591.0 11.7 %fusion.153 = f32[1024,1536]{1,0:T(8,128)S(1)} fusion(bf16[1024,2240]{0,1:T(8,128)(2,1)} %get-tuple-element.76, bf16[2240,1536]{1,0:T(8,128)(2,1)} %bitcast.485), kind=kOutput, calls=%fused_computation.343 | convolution fusion | flops 7046430720 | bytes 17760256 | tf_op jit(solution)/shard_map/dot_general | solution.py:61
  609.0 6.2 bitcast_add_fusion.1
  620.7 6.2 bitcast_add_fusion.2
  631.5 9.1 bitcast_add_fusion.4
  640.6 5.2 dynamic-slice_bitcast_fusion.28
  657.6 6.6 bitcast_add_fusion.3
  669.1 29.9 %collective-permute-done.52 = f32[4,96,2240]{2,1,0:T(8,128)} collective-permute-done((f32[4,96,2240]{2,1,0:T(8,128)}, f32[4,96,2240]{2,1,0:T(8,128)}, u32[]{:S(2)}, u32[]{:S(2)}) %collective-permute-start.52) | collective-permute-done | bytes 3440672 | tf_op jit(solution)/shard_map/ppermute | solution.py:65
  702.0 71.5 %collective-permute-done.50 = f32[4,96,2240]{2,1,0:T(8,128)} collective-permute-done((f32[4,96,2240]{2,1,0:T(8,128)}, f32[4,96,2240]{2,1,0:T(8,128)}, u32[]{:S(2)}, u32[]{:S(2)}) %collective-permute-start.50) | collective-permute-done | bytes 3440672 | tf_op jit(solution)/shard_map/ppermute | solution.py:65
  779.8 5.2 all-to-all-start.4
  785.1 7.4 fusion.67
  798.0 26.4 %all-to-all-done.4 = bf16[4,2,96,2240]{3,2,1,0:T(8,128)(2,1)} async-done(((bf16[4,2,96,2240]{3,2,1,0:T(8,128)(2,1)}), bf16[4,2,96,2240]{3,2,1,0:T(8,128)(2,1)}, u32[]{:S(2)}, u32[]{:S(2)}) %all-to-all-start.4) | async-done | bytes 3440672 | tf_op jit(solution)/shard_map/all_to_all | solution.py:325
  837.8 54.3 %collective-permute-done.40 = f32[256,768]{1,0:T(8,128)S(1)} collective-permute-done((f32[256,768]{1,0:T(8,128)S(1)}, f32[256,768]{1,0:T(8,128)S(1)}, u32[]{:S(2)}, u32[]{:S(2)}) %collective-permute-start.40) | collective-permute-done | bytes 786464 | tf_op jit(solution)/shard_map/ppermute | solution.py:65
  892.1 8.9 collective-permute-done.38
  905.1 3.8 fusion.63
  913.7 4.1 squeeze.232
  920.4 4.2 squeeze.231
  924.7 21.9 %conditional.3 = (bf16[9496,1536]{1,0:T(8,128)(2,1)}) conditional(s32[]{:T(128)} %convert_element_type.238, (s32[20,768]{1,0:T(8,128)S(1)}, f32[16,48,1536]{2,1,0:T(8,128)}, s32[768]{0:T(1024)S(1)}, s32[768]{0:T(1024)S(1)}) %tuple.129, (s32[]{:T(128)}, s32[16,512]{1,0:T(8,128)S(1)}, s32[16,512]{1,0:T(8,128)S(1)}, ...), branch_computations={%region_23.25_spmd, %region_25.27_spmd} | conditional | flops 40000016384 | bytes 366523680 | solution.py:356
  925.4 19.6 %branch_0_fun.1 = bf16[9496,1536]{1,0:T(8,128)(2,1)} custom-call(s32[20]{0:T(128)} %reduce_sum.90.start_ref, s32[768]{0:T(1024)S(1)} %get-tuple-element.44.slot_ref, s32[768]{0:T(1024)S(1)} %get-tuple-element.45.row_ref, f32[768,1536]{1,0:T(8,128)} %bitcast.17.recv_ref), custom_call_target="tpu_custom_call" | custom-call | flops 40000000000 | bytes 40000000 | tf_op jit(solution)/shard_map/cond/branch_0_fun/pallas_call | solution.py:88
  953.1 10.9 %collective-permute-done.48 = f32[96,1536]{1,0:T(8,128)S(1)} collective-permute-done((f32[96,1536]{1,0:T(8,128)S(1)}, f32[96,1536]{1,0:T(8,128)S(1)}, u32[]{:S(2)}, u32[]{:S(2)}) %collective-permute-start.48) | collective-permute-done | bytes 589856 | tf_op jit(solution)/shard_map/ppermute | solution.py:65
  965.8 12.9 %collective-permute-done.46 = f32[96,2048]{1,0:T(8,128)S(1)} collective-permute-done((f32[96,2048]{1,0:T(8,128)S(1)}, f32[96,2048]{1,0:T(8,128)S(1)}, u32[]{:S(2)}, u32[]{:S(2)}) %collective-permute-start.46) | collective-permute-done | bytes 786464 | tf_op jit(solution)/shard_map/ppermute | solution.py:65
  (431 shorter events, 218.6 us)
Async XLA Ops:
  7.2 98.2 %all-gather.5.cloned.1.call-start = ((), (), s32[]{:S(2)}) async-start(), calls=%async_computation.9 | async-start | bytes 6684672 | tf_op jit(solution)/shard_map/all_gather | solution.py:245
  27.1 57.9 %copy-start.65 = (s32[16,512]{1,0:T(8,128)}, s32[16,512]{1,0:T(8,128)S(1)}, u32[]{:S(2)}) copy-start(s32[16,512]{1,0:T(8,128)S(1)} %get-tuple-element.165) | copy-start | bytes 98308
  27.3 57.7 %copy-start.61 = (s32[16,512]{1,0:T(8,128)}, s32[16,512]{1,0:T(8,128)S(1)}, u32[]{:S(2)}) copy-start(s32[16,512]{1,0:T(8,128)S(1)} %broadcast_subtract_fusion) | copy-start | bytes 98308
  27.8 19.6 %copy-start.77 = (s32[16,48]{1,0:T(8,128)}, s32[16,48]{1,0:T(8,128)S(1)}, u32[]{:S(2)}) copy-start(s32[16,48]{1,0:T(8,128)S(1)} %select_reduce_fusion) | copy-start | bytes 9220
  28.3 19.1 %copy-start.88 = (pred[16,48]{1,0:T(8,128)(4,1)}, pred[16,48]{1,0:T(8,128)(4,1)S(1)}, u32[]{:S(2)}) copy-start(pred[16,48]{1,0:T(8,128)(4,1)S(1)} %fusion.88) | copy-start | bytes 2308
  47.4 36.2 %all-to-all-start = ((bf16[16,48,1536]{2,1,0:T(8,128)(2,1)}), bf16[16,48,1536]{2,1,0:T(8,128)(2,1)S(1)}, u32[]{:S(2)}, u32[]{:S(2)}) async-start(bf16[16,48,1536]{2,1,0:T(8,128)(2,1)} %bitcast.24), calls=%async_computation | async-start | bytes 4718592 | tf_op jit(solution)/shard_map/all_to_all | solution.py:227
  51.0 92.4 %all-gather.7.cloned.1.call-start = ((), (), s32[]{:S(2)}) async-start(), calls=%async_computation.10 | async-start | bytes 5013504 | tf_op jit(solution)/shard_map/all_gather | solution.py:246
  54.4 30.6 %copy-start.94 = (s32[512]{0:T(512)}, s32[512]{0:T(512)S(1)}, u32[]{:S(2)}) copy-start(s32[512]{0:T(512)S(1)} %select_reduce_fusion.1) | copy-start | bytes 6148
  90.4 15.0 %copy-start.86 = (f32[512]{0:T(512)}, f32[512]{0:T(512)S(1)}, u32[]{:S(2)}) copy-start(f32[512]{0:T(512)S(1)} %get-tuple-element.75) | copy-start | bytes 6148
  90.4 15.0 %copy-start.13 = (f32[512,1536]{1,0:T(8,128)}, f32[512,1536]{1,0:T(8,128)S(1)}, u32[]{:S(2)}) copy-start(f32[512,1536]{1,0:T(8,128)S(1)} %get-tuple-element.74) | copy-start | bytes 9437188
  90.4 71.3 %collective-permute-start.33 = (bf16[512,1536]{1,0:T(8,128)(2,1)}, bf16[512,1536]{1,0:T(8,128)(2,1)}, u32[]{:S(2)}, u32[]{:S(2)}) collective-permute-start(bf16[512,1536]{1,0:T(8,128)(2,1)} %bitcast.494), channel_id=1, source_target_pairs={{0,4},{4,0},{1,5},{5,1},{2,6},{6,2},{3,7},{7,3},{8,12},{12,8},{9,1... | collective-permute-start | bytes 4718600 | tf_op jit(solution)/shard_map/ppermute | solution.py:65
  92.1 72.8 %collective-permute-start.32 = (bf16[512,1536]{1,0:T(8,128)(2,1)}, bf16[512,1536]{1,0:T(8,128)(2,1)}, u32[]{:S(2)}, u32[]{:S(2)}) collective-permute-start(bf16[512,1536]{1,0:T(8,128)(2,1)} %bitcast.495), channel_id=1, source_target_pairs={{0,8},{8,0},{1,9},{9,1},{2,10},{10,2},{3,11},{11,3},{4,12},{12,4},... | collective-permute-start | bytes 4718600 | tf_op jit(solution)/shard_map/ppermute | solution.py:65
  93.7 102.9 %collective-permute-start.36 = (bf16[1,560,1536]{2,1,0:T(8,128)(2,1)}, bf16[1,560,1536]{2,1,0:T(8,128)(2,1)}, u32[]{:S(2)}, u32[]{:S(2)}) collective-permute-start(bf16[1,560,1536]{2,1,0:T(8,128)(2,1)} %bitcast.506), channel_id=1, source_target_pairs={{0,2},{2,0},{1,3},{3,1},{4,6},{6,4},{5,7},{7,5},{8,10},{10,8},{9,1... | collective-permute-start | bytes 5160968 | tf_op jit(solution)/shard_map/ppermute | solution.py:65
  96.9 58.5 %all-to-all-start.2 = ((bf16[4,96,2240]{2,1,0:T(8,128)(2,1)}), bf16[4,96,2240]{2,1,0:T(8,128)(2,1)}, u32[]{:S(2)}, u32[]{:S(2)}) async-start(bf16[4,96,2240]{2,1,0:T(8,128)(2,1)} %pad_maximum_fusion.4), calls=%async_computation.2 | async-start | bytes 3538944 | tf_op jit(solution)/shard_map/all_to_all | solution.py:257
  101.9 47.3 %copy-start.72 = (f32[1536]{0:T(1024)}, f32[1536]{0:T(1024)S(1)}, u32[]{:S(2)}) copy-start(f32[1536]{0:T(1024)S(1)} %mul.383) | copy-start | bytes 18436
  102.0 33.3 %copy-start.37 = (pred[512,512]{0,1:T(8,128)(4,1)}, pred[512,512]{0,1:T(8,128)(4,1)S(1)}, u32[]{:S(2)}) copy-start(pred[512,512]{0,1:T(8,128)(4,1)S(1)} %iota_compare_fusion.4) | copy-start | bytes 786436
  149.1 12.6 %copy-start.90 = (f32[512]{0:T(512)}, f32[512]{0:T(512)S(1)}, u32[]{:S(2)}) copy-start(f32[512]{0:T(512)S(1)} %get-tuple-element.228) | copy-start | bytes 6148
  149.1 12.6 %copy-start.82 = (f32[512]{0:T(512)}, f32[512]{0:T(512)S(1)}, u32[]{:S(2)}) copy-start(f32[512]{0:T(512)S(1)} %fusion.130) | copy-start | bytes 6148
  155.4 34.7 %all-to-all-start.1 = ((bf16[4,96,2240]{2,1,0:T(8,128)(2,1)}), bf16[4,96,2240]{2,1,0:T(8,128)(2,1)S(1)}, u32[]{:S(2)}, u32[]{:S(2)}) async-start(bf16[4,96,2240]{2,1,0:T(8,128)(2,1)} %pad_maximum_fusion.3), calls=%async_computation.1 | async-start | bytes 3538944 | tf_op jit(solution)/shard_map/all_to_all | solution.py:257
  159.0 107.8 %all-gather.11.cloned.1.call-start = ((), (), s32[]{:S(2)}) async-start(), calls=%async_computation.12 | async-start | bytes 3932160 | tf_op jit(solution)/shard_map/all_gather | solution.py:289
  161.7 174.9 %all-gather.9.cloned.1.call-start = ((), (), s32[]{:S(2)}) async-start(), calls=%async_computation.11 | async-start | bytes 3932160 | tf_op jit(solution)/shard_map/all_gather | solution.py:289
  162.9 46.1 %collective-permute-start.35 = (bf16[512,768]{1,0:T(8,128)(2,1)S(1)}, bf16[512,768]{1,0:T(8,128)(2,1)}, u32[]{:S(2)}, u32[]{:S(2)}) collective-permute-start(bf16[512,768]{1,0:T(8,128)(2,1)S(1)} %slice.185), channel_id=1, source_target_pairs={{0,8},{8,0},{1,9},{9,1},{2,10},{10,2},{3,11},{11,3},{4,12},{12,4},... | collective-permute-start | bytes 2359304 | tf_op jit(solution)/shard_map/ppermute | solution.py:65
  167.0 43.0 %collective-permute-start.34 = (bf16[512,768]{1,0:T(8,128)(2,1)}, bf16[512,768]{1,0:T(8,128)(2,1)}, u32[]{:S(2)}, u32[]{:S(2)}) collective-permute-start(bf16[512,768]{1,0:T(8,128)(2,1)} %slice.184), channel_id=1, source_target_pairs={{0,4},{4,0},{1,5},{5,1},{2,6},{6,2},{3,7},{7,3},{8,12},{12,8},{9,1... | collective-permute-start | bytes 2359304 | tf_op jit(solution)/shard_map/ppermute | solution.py:65
  172.8 85.4 %collective-permute-start.31 = (bf16[4,96,2240]{2,1,0:T(8,128)(2,1)}, bf16[4,96,2240]{2,1,0:T(8,128)(2,1)}, u32[]{:S(2)}, u32[]{:S(2)}) collective-permute-start(bf16[4,96,2240]{2,1,0:T(8,128)(2,1)} %all-to-all-done.2.own_ref), channel_id=1, source_target_pairs={{0,2},{2,0},{1,3},{3,1},{4,6},{6,4},{5,7},{7,5},{8,10},{10,8},{9,1... | collective-permute-start | bytes 5160968 | tf_op jit(solution)/shard_map/ppermute | solution.py:65
  190.1 14.7 %copy-start.22 = (bf16[4,96,2240]{2,1,0:T(8,128)(2,1)}, bf16[4,96,2240]{2,1,0:T(8,128)(2,1)S(1)}, u32[]{:S(2)}) copy-start(bf16[4,96,2240]{2,1,0:T(8,128)(2,1)S(1)} %all-to-all-done.1.own_ref) | copy-start | bytes 5160964
  190.1 59.7 %collective-permute-start.30 = (bf16[4,96,2240]{2,1,0:T(8,128)(2,1)S(1)}, bf16[4,96,2240]{2,1,0:T(8,128)(2,1)}, u32[]{:S(2)}, u32[]{:S(2)}) collective-permute-start(bf16[4,96,2240]{2,1,0:T(8,128)(2,1)S(1)} %all-to-all-done.1.own_ref), channel_id=1, source_target_pairs={{0,2},{2,0},{1,3},{3,1},{4,6},{6,4},{5,7},{7,5},{8,10},{10,8},{9,1... | collective-permute-start | bytes 5160968 | tf_op jit(solution)/shard_map/ppermute | solution.py:65
  266.7 218.1 %reduce-scatter.7.cloned.1.call-start = ((), (), s32[]{:S(2)}) async-start(), calls=%async_computation.14 | async-start | bytes 7864320 | tf_op jit(solution)/shard_map/reduce_scatter | solution.py:297
  266.8 13.8 %copy-start.39 = (bf16[1024,1536]{1,0:T(8,128)(2,1)S(1)}, bf16[1024,1536]{1,0:T(8,128)(2,1)}, u32[]{:S(2)}) copy-start(bf16[1024,1536]{1,0:T(8,128)(2,1)} %all-gather.11.cloned.1.call-done) | copy-start | bytes 9437188
  300.9 11.9 %copy-start.101 = (bf16[1024,2240]{0,1:T(8,128)(2,1)S(1)}, bf16[1024,2240]{0,1:T(8,128)(2,1)}, u32[]{:S(2)}) copy-start(bf16[1024,2240]{0,1:T(8,128)(2,1)} %get-tuple-element.82) | copy-start | bytes 13762564
  324.6 163.0 %reduce-scatter.5.cloned.1.call-start = ((), (), s32[]{:S(2)}) async-start(), calls=%async_computation.13 | async-start | bytes 7864320 | tf_op jit(solution)/shard_map/reduce_scatter | solution.py:297
  395.5 551.1 %reduce-scatter.11.cloned.1.call-start = ((), (), s32[]{:S(2)}) async-start(), calls=%async_computation.16 | async-start | bytes 5898240 | tf_op jit(solution)/shard_map/reduce_scatter | solution.py:318
  420.2 226.9 %collective-permute-start.43 = (f32[2,256,768]{2,1,0:T(8,128)}, f32[2,256,768]{2,1,0:T(8,128)}, u32[]{:S(2)}, u32[]{:S(2)}) collective-permute-start(f32[2,256,768]{2,1,0:T(8,128)} %slice.196), channel_id=1, source_target_pairs={{0,4},{4,0},{1,5},{5,1},{2,6},{6,2},{3,7},{7,3},{8,12},{12,8},{9,1... | collective-permute-start | bytes 4718600 | tf_op jit(solution)/shard_map/ppermute | solution.py:65
  422.1 20.1 %copy-start.41 = (bf16[2048,1536]{1,0:T(8,128)(2,1)}, bf16[2048,1536]{1,0:T(8,128)(2,1)S(1)}, u32[]{:S(2)}) copy-start(bf16[2048,1536]{1,0:T(8,128)(2,1)S(1)} %constant_dynamic-update-slice_fusion.20) | copy-start | bytes 18874372
  442.2 38.6 %slice-start.11 = ((s8[4587520]{0:T(1024)(128)(4,1)}), s8[4194304]{0:T(1024)(128)(4,1)S(1)}, s32[]{:S(2)}) async-start(s8[4587520]{0:T(1024)(128)(4,1)} %bitcast.498), calls=%async_computation.28 | async-start | bytes 8388608
  442.2 38.6 %slice-start.13 = ((s8[4587520]{0:T(1024)(128)(4,1)}), s8[4194304]{0:T(1024)(128)(4,1)S(1)}, s32[]{:S(2)}) async-start(s8[4587520]{0:T(1024)(128)(4,1)} %bitcast.500), calls=%async_computation.30 | async-start | bytes 8388608
  452.0 28.8 %slice-start.12 = ((s8[4587520]{0:T(1024)(128)(4,1)}), s8[393216]{0:T(1024)(128)(4,1)S(1)}, s32[]{:S(2)}) async-start(s8[4587520]{0:T(1024)(128)(4,1)} %bitcast.498), calls=%async_computation.29 | async-start | bytes 786432
  452.0 28.8 %slice-start.14 = ((s8[4587520]{0:T(1024)(128)(4,1)}), s8[393216]{0:T(1024)(128)(4,1)S(1)}, s32[]{:S(2)}) async-start(s8[4587520]{0:T(1024)(128)(4,1)} %bitcast.500), calls=%async_computation.31 | async-start | bytes 786432
  452.0 155.6 %collective-permute-start.51 = (f32[4,2,96,2240]{3,2,1,0:T(8,128)}, f32[4,2,96,2240]{3,2,1,0:T(8,128)}, u32[]{:S(2)}, u32[]{:S(2)}) collective-permute-start(f32[4,2,96,2240]{3,2,1,0:T(8,128)} %dynamic-slice_bitcast_fusion.15), channel_id=1, source_target_pairs={{0,1},{1,0},{2,3},{3,2},{4,5},{5,4},{6,7},{7,6},{8,9},{9,8},{10,11... | collective-permute-start | bytes 20643848 | tf_op jit(solution)/shard_map/ppermute | solution.py:65
  480.5 138.8 %collective-permute-start.49 = (f32[4,2,96,2240]{3,2,1,0:T(8,128)}, f32[4,2,96,2240]{3,2,1,0:T(8,128)}, u32[]{:S(2)}, u32[]{:S(2)}) collective-permute-start(f32[4,2,96,2240]{3,2,1,0:T(8,128)} %dynamic-slice_bitcast_fusion.16), channel_id=1, source_target_pairs={{0,1},{1,0},{2,3},{3,2},{4,5},{5,4},{6,7},{7,6},{8,9},{9,8},{10,11... | collective-permute-start | bytes 20643848 | tf_op jit(solution)/shard_map/ppermute | solution.py:65
  527.4 31.8 %collective-permute-start.47 = (f32[4,2,96,1536]{3,2,1,0:T(8,128)}, f32[4,2,96,1536]{3,2,1,0:T(8,128)}, u32[]{:S(2)}, u32[]{:S(2)}) collective-permute-start(f32[4,2,96,1536]{3,2,1,0:T(8,128)} %dynamic-slice_bitcast_fusion.19), channel_id=1, source_target_pairs={{0,1},{1,0},{2,3},{3,2},{4,5},{5,4},{6,7},{7,6},{8,9},{9,8},{10,11... | collective-permute-start | bytes 14155784 | tf_op jit(solution)/shard_map/ppermute | solution.py:65
  559.1 71.9 %collective-permute-start.45 = (f32[4,2,96,2048]{3,2,1,0:T(8,128)}, f32[4,2,96,2048]{3,2,1,0:T(8,128)}, u32[]{:S(2)}, u32[]{:S(2)}) collective-permute-start(f32[4,2,96,2048]{3,2,1,0:T(8,128)} %dynamic-slice_bitcast_fusion.18), channel_id=1, source_target_pairs={{0,1},{1,0},{2,3},{3,2},{4,5},{5,4},{6,7},{7,6},{8,9},{9,8},{10,11... | collective-permute-start | bytes 18874376 | tf_op jit(solution)/shard_map/ppermute | solution.py:65
  564.6 385.3 %reduce-scatter.9.cloned.1.call-start = ((), (), s32[]{:S(2)}) async-start(), calls=%async_computation.15 | async-start | bytes 7864320 | tf_op jit(solution)/shard_map/reduce_scatter | solution.py:318
  590.5 65.1 %collective-permute-start.53 = (f32[2,560,1536]{2,1,0:T(8,128)}, f32[2,560,1536]{2,1,0:T(8,128)}, u32[]{:S(2)}, u32[]{:S(2)}) collective-permute-start(f32[2,560,1536]{2,1,0:T(8,128)} %dynamic-slice_bitcast_fusion.17), channel_id=1, source_target_pairs={{0,1},{1,0},{2,3},{3,2},{4,5},{5,4},{6,7},{7,6},{8,9},{9,8},{10,11... | collective-permute-start | bytes 20643848 | tf_op jit(solution)/shard_map/ppermute | solution.py:65
  607.6 46.3 %collective-permute-start.41 = (f32[2,256,768]{2,1,0:T(8,128)S(1)}, f32[2,256,768]{2,1,0:T(8,128)S(1)}, u32[]{:S(2)}, u32[]{:S(2)}) collective-permute-start(f32[2,256,768]{2,1,0:T(8,128)S(1)} %copy-done.43), channel_id=1, source_target_pairs={{0,8},{8,0},{1,9},{9,1},{2,10},{10,2},{3,11},{11,3},{4,12},{12,4},... | collective-permute-start | bytes 4718600 | tf_op jit(solution)/shard_map/ppermute | solution.py:65
  619.2 79.7 %collective-permute-start.52 = (f32[4,96,2240]{2,1,0:T(8,128)}, f32[4,96,2240]{2,1,0:T(8,128)}, u32[]{:S(2)}, u32[]{:S(2)}) collective-permute-start(f32[4,96,2240]{2,1,0:T(8,128)} %dynamic-slice_bitcast_fusion.20), channel_id=1, source_target_pairs={{0,2},{2,0},{1,3},{3,1},{4,6},{6,4},{5,7},{7,5},{8,10},{10,8},{9,1... | collective-permute-start | bytes 10321928 | tf_op jit(solution)/shard_map/ppermute | solution.py:65
  631.0 142.5 %collective-permute-start.50 = (f32[4,96,2240]{2,1,0:T(8,128)}, f32[4,96,2240]{2,1,0:T(8,128)}, u32[]{:S(2)}, u32[]{:S(2)}) collective-permute-start(f32[4,96,2240]{2,1,0:T(8,128)} %dynamic-slice_bitcast_fusion.21), channel_id=1, source_target_pairs={{0,2},{2,0},{1,3},{3,1},{4,6},{6,4},{5,7},{7,5},{8,10},{10,8},{9,1... | collective-permute-start | bytes 10321928 | tf_op jit(solution)/shard_map/ppermute | solution.py:65
  647.1 180.9 %collective-permute-start.39 = (f32[2,256,768]{2,1,0:T(8,128)}, f32[2,256,768]{2,1,0:T(8,128)}, u32[]{:S(2)}, u32[]{:S(2)}) collective-permute-start(f32[2,256,768]{2,1,0:T(8,128)} %slice.190), channel_id=1, source_target_pairs={{0,4},{4,0},{1,5},{5,1},{2,6},{6,2},{3,7},{7,3},{8,12},{12,8},{9,1... | collective-permute-start | bytes 4718600 | tf_op jit(solution)/shard_map/ppermute | solution.py:65
  653.9 177.9 %collective-permute-start.37 = (f32[2,256,768]{2,1,0:T(8,128)}, f32[2,256,768]{2,1,0:T(8,128)}, u32[]{:S(2)}, u32[]{:S(2)}) collective-permute-start(f32[2,256,768]{2,1,0:T(8,128)} %slice.188), channel_id=1, source_target_pairs={{0,8},{8,0},{1,9},{9,1},{2,10},{10,2},{3,11},{11,3},{4,12},{12,4},... | collective-permute-start | bytes 4718600 | tf_op jit(solution)/shard_map/ppermute | solution.py:65
  654.6 45.1 %slice-start.3 = ((s8[7077888]{0:T(1024)(128)(4,1)}), s8[4194304]{0:T(1024)(128)(4,1)S(1)}, s32[]{:S(2)}) async-start(s8[7077888]{0:T(1024)(128)(4,1)} %bitcast.455), calls=%async_computation.20 | async-start | bytes 8388608
  655.6 44.1 %slice-start.4 = ((s8[7077888]{0:T(1024)(128)(4,1)}), s8[2883584]{0:T(1024)(128)(4,1)S(1)}, s32[]{:S(2)}) async-start(s8[7077888]{0:T(1024)(128)(4,1)} %bitcast.455), calls=%async_computation.21 | async-start | bytes 5767168
  656.0 179.3 %collective-permute-start.44 = (f32[256,768]{1,0:T(8,128)}, f32[256,768]{1,0:T(8,128)}, u32[]{:S(2)}, u32[]{:S(2)}) collective-permute-start(f32[256,768]{1,0:T(8,128)} %dynamic-slice_bitcast_fusion.32), channel_id=1, source_target_pairs={{0,8},{8,0},{1,9},{9,1},{2,10},{10,2},{3,11},{11,3},{4,12},{12,4},... | collective-permute-start | bytes 2359304 | tf_op jit(solution)/shard_map/ppermute | solution.py:65
  664.2 110.7 %slice-start.5 = ((s8[7077888]{0:T(1024)(128)(4,1)}), s8[4194304]{0:T(1024)(128)(4,1)S(1)}, s32[]{:S(2)}) async-start(s8[7077888]{0:T(1024)(128)(4,1)} %bitcast.457), calls=%async_computation.22 | async-start | bytes 8388608
  669.1 105.9 %slice-start.6 = ((s8[7077888]{0:T(1024)(128)(4,1)}), s8[2883584]{0:T(1024)(128)(4,1)S(1)}, s32[]{:S(2)}) async-start(s8[7077888]{0:T(1024)(128)(4,1)} %bitcast.457), calls=%async_computation.23 | async-start | bytes 5767168
  698.9 137.6 %collective-permute-start.42 = (f32[256,768]{1,0:T(8,128)}, f32[256,768]{1,0:T(8,128)}, u32[]{:S(2)}, u32[]{:S(2)}) collective-permute-start(f32[256,768]{1,0:T(8,128)} %dynamic-slice_bitcast_fusion.33), channel_id=1, source_target_pairs={{0,4},{4,0},{1,5},{5,1},{2,6},{6,2},{3,7},{7,3},{8,12},{12,8},{9,1... | collective-permute-start | bytes 2359304 | tf_op jit(solution)/shard_map/ppermute | solution.py:65
  773.5 130.8 %collective-permute-start.54 = (f32[560,1536]{1,0:T(8,128)}, f32[560,1536]{1,0:T(8,128)}, u32[]{:S(2)}, u32[]{:S(2)}) collective-permute-start(f32[560,1536]{1,0:T(8,128)} %dynamic-slice_bitcast_fusion.22), channel_id=1, source_target_pairs={{0,2},{2,0},{1,3},{3,1},{4,6},{6,4},{5,7},{7,5},{8,10},{10,8},{9,1... | collective-permute-start | bytes 10321928 | tf_op jit(solution)/shard_map/ppermute | solution.py:65
  779.8 44.6 %all-to-all-start.4 = ((bf16[4,2,96,2240]{3,2,1,0:T(8,128)(2,1)}), bf16[4,2,96,2240]{3,2,1,0:T(8,128)(2,1)}, u32[]{:S(2)}, u32[]{:S(2)}) async-start(bf16[4,2,96,2240]{3,2,1,0:T(8,128)(2,1)} %copy.201), calls=%async_computation.8 | async-start | bytes 7077888 | tf_op jit(solution)/shard_map/all_to_all | solution.py:325
  798.0 30.0 %copy-start.21 = (f32[2,256,1536]{2,1,0:T(8,128)S(1)}, f32[2,256,1536]{2,1,0:T(8,128)}, u32[]{:S(2)}) copy-start(f32[2,256,1536]{2,1,0:T(8,128)} %get-tuple-element.189) | copy-start | bytes 9437188
  824.4 100.2 %all-to-all-start.3 = ((f32[16,48,1536]{2,1,0:T(8,128)}), f32[16,48,1536]{2,1,0:T(8,128)}, u32[]{:S(2)}, u32[]{:S(2)}) async-start(f32[16,48,1536]{2,1,0:T(8,128)} %select_select_fusion.1), calls=%async_computation.5 | async-start | bytes 9437184 | tf_op jit(solution)/shard_map/all_to_all | solution.py:342
  829.9 62.2 %collective-permute-start.40 = (f32[256,768]{1,0:T(8,128)S(1)}, f32[256,768]{1,0:T(8,128)S(1)}, u32[]{:S(2)}, u32[]{:S(2)}) collective-permute-start(f32[256,768]{1,0:T(8,128)S(1)} %dynamic-slice_bitcast_fusion.34), channel_id=1, source_target_pairs={{0,8},{8,0},{1,9},{9,1},{2,10},{10,2},{3,11},{11,3},{4,12},{12,4},... | collective-permute-start | bytes 2359304 | tf_op jit(solution)/shard_map/ppermute | solution.py:65
  833.7 67.3 %collective-permute-start.38 = (f32[256,768]{1,0:T(8,128)S(1)}, f32[256,768]{1,0:T(8,128)S(1)}, u32[]{:S(2)}, u32[]{:S(2)}) collective-permute-start(f32[256,768]{1,0:T(8,128)S(1)} %dynamic-slice_bitcast_fusion.35), channel_id=1, source_target_pairs={{0,4},{4,0},{1,5},{5,1},{2,6},{6,2},{3,7},{7,3},{8,12},{12,8},{9,1... | collective-permute-start | bytes 2359304 | tf_op jit(solution)/shard_map/ppermute | solution.py:65
  946.6 34.2 %copy-start.1 = (bf16[96,12,128]{2,0,1:T(8,128)(2,1)S(1)}, bf16[96,12,128]{2,0,1:T(8,128)(2,1)}, u32[]{:S(2)}) copy-start(bf16[96,12,128]{2,0,1:T(8,128)(2,1)} %param.25) | copy-start | bytes 884740
  947.8 16.2 %collective-permute-start.48 = (f32[96,1536]{1,0:T(8,128)S(1)}, f32[96,1536]{1,0:T(8,128)S(1)}, u32[]{:S(2)}, u32[]{:S(2)}) collective-permute-start(f32[96,1536]{1,0:T(8,128)S(1)} %dynamic-slice_bitcast_fusion.36), channel_id=1, source_target_pairs={{0,2},{2,0},{1,3},{3,1},{4,6},{6,4},{5,7},{7,5},{8,10},{10,8},{9,1... | collective-permute-start | bytes 1769480 | tf_op jit(solution)/shard_map/ppermute | solution.py:65
  949.9 28.8 %copy-start.42 = (f32[192,2048]{1,0:T(8,128)S(1)}, f32[192,2048]{1,0:T(8,128)}, u32[]{:S(2)}) copy-start(f32[192,2048]{1,0:T(8,128)} %reduce-scatter.9.cloned.1.call-done) | copy-start | bytes 4718596
  951.2 27.5 %collective-permute-start.46 = (f32[96,2048]{1,0:T(8,128)S(1)}, f32[96,2048]{1,0:T(8,128)S(1)}, u32[]{:S(2)}, u32[]{:S(2)}) collective-permute-start(f32[96,2048]{1,0:T(8,128)S(1)} %dynamic-slice_bitcast_fusion.31), channel_id=1, source_target_pairs={{0,2},{2,0},{1,3},{3,1},{4,6},{6,4},{5,7},{7,5},{8,10},{10,8},{9,1... | collective-permute-start | bytes 2359304 | tf_op jit(solution)/shard_map/ppermute | solution.py:65
  (82 other events, 437.4 us)
Sparse Core Ops, SparseCore 0:
  10.2 44.9 all-gather.4
  57.5 56.2 all-gather.6
  162.2 59.9 all-gather.10
  266.9 38.6 all-gather.8
  324.7 64.6 reduce-scatter.6
  395.6 91.8 reduce-scatter.4
  564.7 59.6 reduce-scatter.10
  640.8 112.3 reduce-scatter.8
where the time goes:
time: 999 us; the launch traced here: 988 us
  matrix products  301 us (30%)
  waiting for transfers between devices  296 us (30%)
  local copies, waits for them, and re-layouts  166 us (17%)
  other arithmetic  106 us (11%)
  Pallas kernels  53.9 us (5%)
  starting transfers between devices  45.3 us (5%)
  between operations  17.1 us (2%)
    dot_general x24, matrix products, dot(): lax.dot_general(a, b, (((ca,), (cb,)), ((), ())), preferred_element_type=...  257 us
    ppermute x25, waiting for transfers between devices, flip(): return lax.ppermute(a, axis, [(0, 1), (1, 0)])  219 us
    add x13, other arithmetic, add_flip(): return keep + got_half  41.6 us
    squeeze x18, local copies, waits for them, and re-layouts, pick_dim(): return lax.dynamic_index_in_dim(a, index, dim, keepdims=False)  40.3 us
    unnamed x219, local copies, waits for them, and re-layouts  36.4 us
    all_to_all x1, waiting for transfers between devices, step(): got = lax.all_to_all(sent, ALL, 0, 0, tiled=True)  29.2 us
    all_to_all x1, waiting for transfers between devices, step(): lax.all_to_all(jnp.stack([g_gate, g_up], axis=1), PLANE, 0, 0, tiled=True)  26.4 us
    pallas_call x3, Pallas kernels, gather_xc(): pl.pallas_call(pair_kernel, out_shape=jax.ShapeDtypeStruct((a, 2, 2, r, n...  25.1 us
  transfers between devices with their start and end apart: 38, of which 15 were waited for; matrix products, arithmetic and copies ran while one was open for 54% of the time, Pallas kernels for 5%

commit v1 on v0

--- a/solution.py
+++ b/solution.py
@@ -123,6 +123,24 @@
         )
         copies[-1].start()
     out_ref[me] = in_ref[...]
+    for copy in copies:
+        copy.wait()
+
+
+def swap_kernel(in_ref, out_ref, send_sem, recv_sem):
+    me = lax.axis_index(ALL)
+    enter_all()
+    copies = []
+    for m in range(N_DEV - 1, 0, -1):
+        z, y, x, c = flipped(m)
+        to = ((z * 2 + y) * 2 + x) * 2 + c
+        copies.append(
+            pltpu.make_async_remote_copy(
+                src_ref=in_ref.at[to], dst_ref=out_ref.at[me], send_sem=send_sem.at[m], recv_sem=recv_sem.at[m], device_id=(z, y, x, c), device_id_type=MESH
+            )
+        )
+        copies[-1].start()
+    out_ref[me] = in_ref[me]
     for copy in copies:
         copy.wait()
 
@@ -224,7 +242,7 @@
         pick = (slot_tok[:, None] == jnp.arange(N_DEV * SLOTS)[None, :]).astype(BF16)
 
         sent = table.at[fetch_row.reshape(-1)].get(mode="promise_in_bounds").reshape(N_DEV, SLOTS, dim)
-        got = lax.all_to_all(sent, ALL, 0, 0, tiled=True)
+        got = exchange(swap_kernel, sent, sent.shape, 1, 100_000_000)
         emb_fast = dot(pick, got.reshape(-1, dim), 1, 0).astype(BF16)
 
         def ring(k):

time: 999 us -> 1010 us (1.011)
  Pallas kernels: 53.9 us -> 95.1 us
  waiting for transfers between devices: 296 us -> 263 us
    pallas_call x1 -> x2, Pallas kernels: 9.22 us -> 50.4 us  [exchange(): pl.pallas_call(kernel, out_shape=jax.ShapeDtypeStruct(out_shape, array.dt...]
    all_to_all x1 -> x0, waiting for transfers between devices: 29.2 us -> none  [step(): got = lax.all_to_all(sent, ALL, 0, 0, tiled=True)]
  transfers between devices with their start and end apart: 38 -> 37, of which waited for: 15 -> 13; matrix products, arithmetic and copies ran while one was open for 54% -> 54% of each run, Pallas kernels for 5% -> 10%
where the time goes in v1:
time: 1010 us; the launch traced here: 998 us
  matrix products  303 us (30%)
  waiting for transfers between devices  263 us (26%)
  local copies, waits for them, and re-layouts  167 us (17%)
  other arithmetic  108 us (11%)
  Pallas kernels  95.1 us (9%)
  starting transfers between devices  43.4 us (4%)
  between operations  17.1 us (2%)
    dot_general x24, matrix products, dot(): lax.dot_general(a, b, (((ca,), (cb,)), ((), ())), preferred_element_type=...  259 us
    ppermute x25, waiting for transfers between devices, flip(): return lax.ppermute(a, axis, [(0, 1), (1, 0)])  218 us
    pallas_call x2, Pallas kernels, exchange(): pl.pallas_call(kernel, out_shape=jax.ShapeDtypeStruct(out_shape, array.dt...  50.4 us
    add x13, other arithmetic, add_flip(): return keep + got_half  41.7 us
    squeeze x18, local copies, waits for them, and re-layouts, pick_dim(): return lax.dynamic_index_in_dim(a, index, dim, keepdims=False)  40.3 us
    unnamed x219, local copies, waits for them, and re-layouts  35.9 us
    all_to_all x1, waiting for transfers between devices, step(): lax.all_to_all(jnp.stack([g_gate, g_up], axis=1), PLANE, 0, 0, tiled=True)  26.4 us
    ppermute x25, starting transfers between devices, flip(): return lax.ppermute(a, axis, [(0, 1), (1, 0)])  25.3 us
  transfers between devices with their start and end apart: 37, of which 13 were waited for; matrix products, arithmetic and copies ran while one was open for 54% of the time, Pallas kernels for 10%

profile of v1, /device:TPU:0, one launch (start us, length us, event | category | flops | bytes accessed | tf_op | source)
XLA Modules:
  0.0 997.9 jit_solution(7288506478169431434)
XLA Ops:
  15.9 9.5 shard_map.239
  26.3 4.2 and_reduce_fusion
  33.6 20.0 %gather_fusion.2 = bf16[768,1536]{1,0:T(8,128)(2,1)} fusion(bf16[9496,1536]{1,0:T(8,128)(2,1)} %param.22, s32[1024]{0:T(1024)S(1)} %pad_clamp_fusion.1), kind=kCustom, calls=%fused_computation.2 | custom fusion | bytes 4721664 | tf_op jit(solution)/shard_map/gather | solution.py:244
  53.5 40.8 %shard_map.240 = bf16[16,48,1536]{2,1,0:T(8,128)(2,1)} custom-call(bf16[16,48,1536]{2,1,0:T(8,128)(2,1)} %bitcast.474), custom_call_target="tpu_custom_call" | custom-call | flops 100000000 | bytes 2359296 | tf_op jit(solution)/shard_map/pallas_call | solution.py:149
  98.2 5.4 conditional.2
  109.1 4.8 all-to-all-start.1
  117.6 5.6 fusion.145
  149.6 6.0 fusion.80
  155.6 5.7 fusion.72
  164.0 4.2 all-to-all-start
  184.0 15.4 %all-to-all-done.own_ref = bf16[4,96,2240]{2,1,0:T(8,128)(2,1)S(1)} async-done(((bf16[4,96,2240]{2,1,0:T(8,128)(2,1)}), bf16[4,96,2240]{2,1,0:T(8,128)(2,1)S(1)}, u32[]{:S(2)}, u32[]{:S(2)}) %all-to-all-start) | async-done | bytes 1720352 | tf_op jit(solution)/shard_map/all_to_all | solution.py:275
  206.7 8.2 shard_map.243
  221.3 5.6 fusion.146
  227.0 8.9 convolution_convert_fusion
  235.9 23.0 %collective-permute-done.30.far_ref = bf16[4,96,2240]{2,1,0:T(8,128)(2,1)} collective-permute-done((bf16[4,96,2240]{2,1,0:T(8,128)(2,1)S(1)}, bf16[4,96,2240]{2,1,0:T(8,128)(2,1)}, u32[]{:S(2)}, u32[]{:S(2)}) %collective-permute-start.30) | collective-permute-done | bytes 1720352 | tf_op jit(solution)/shard_map/ppermute | solution.py:65
  258.8 8.4 shard_map.241
  267.3 8.4 shard_map.242
  275.8 13.5 %fusion.154 = f32[1024,2240]{0,1:T(8,128)} fusion(bf16[1024,1536]{1,0:T(8,128)(2,1)} %all-gather.11.cloned.1.call-done, bf16[1536,2240]{1,0:T(8,128)(2,1)} %bitcast.480), kind=kOutput, calls=%fused_computation.344 | convolution fusion | flops 7046430720 | bytes 19202048 | tf_op jit(solution)/shard_map/dot_general | solution.py:61
  289.4 20.3 %fusion.38 = (bf16[1024,2240]{0,1:T(8,128)(2,1)}, bf16[1024,2240]{0,1:T(8,128)(2,1)}, bf16[1024,2240]{0,1:T(8,128)(2,1)}) fusion(f32[1024,2240]{0,1:T(8,128)} %fusion.154, bf16[1024,2240]{0,1:T(8,128)(2,1)} %convolution_convert_fusion, bf16[1024,1536]{1,0:T(8,128)(2,1)S(1)} %copy-done.39, bf16[1536,2240]{1,0:T(8,128)(2,1)} %bitcast.476), kind=kOutput, calls=%fused_computation.99 | convolution fusion | flops 7085424640 | bytes 37552128 | tf_op jit(solution)/shard_map/dot_general | solution.py:61
  309.7 11.9 %fusion.157 = f32[1024,1536]{1,0:T(8,128)S(1)} fusion(bf16[1024,2240]{0,1:T(8,128)(2,1)} %get-tuple-element.83, bf16[1536,2240]{1,0:T(8,128)(2,1)} %bitcast.481), kind=kOutput, calls=%fused_computation.347 | convolution fusion | flops 7046430720 | bytes 17760256 | tf_op jit(solution)/shard_map/dot_general | solution.py:61
  321.6 11.8 %convolution_add_fusion = f32[1024,1536]{1,0:T(8,128)} fusion(f32[1024,1536]{1,0:T(8,128)S(1)} %fusion.157, bf16[1024,2240]{0,1:T(8,128)(2,1)S(1)} %copy-done.101, bf16[1536,2240]{1,0:T(8,128)(2,1)} %bitcast.477), kind=kOutput, calls=%fused_computation.138 | convolution fusion | flops 7048003584 | bytes 24051712 | tf_op jit(solution)/shard_map/dot_general | solution.py:61
  333.4 11.9 %convolution_convert_fusion.1 = bf16[1024,2240]{0,1:T(8,128)(2,1)} fusion(bf16[1024,1536]{1,0:T(8,128)(2,1)} %bitcast.504, bf16[2240,1536]{1,0:T(8,128)(2,1)} %bitcast.484), kind=kOutput, calls=%fused_computation.128 | convolution fusion | flops 7048724480 | bytes 14614528 | tf_op jit(solution)/shard_map/dot_general | solution.py:61
  345.3 13.4 %fusion.152 = f32[1024,2240]{0,1:T(8,128)} fusion(bf16[1024,1536]{1,0:T(8,128)(2,1)} %all-gather.9.cloned.1.call-done, bf16[1536,2240]{1,0:T(8,128)(2,1)} %bitcast.482), kind=kOutput, calls=%fused_computation.342 | convolution fusion | flops 7046430720 | bytes 19202048 | tf_op jit(solution)/shard_map/dot_general | solution.py:61
  358.7 22.4 %fusion.35 = (bf16[1024,2240]{0,1:T(8,128)(2,1)}, bf16[1024,2240]{0,1:T(8,128)(2,1)}, bf16[1024,2240]{0,1:T(8,128)(2,1)}) fusion(f32[1024,2240]{0,1:T(8,128)} %fusion.152, bf16[1024,2240]{0,1:T(8,128)(2,1)} %convolution_convert_fusion.1, bf16[1024,1536]{1,0:T(8,128)(2,1)} %all-gather.9.cloned.1.call-done, bf16[1536,2240]{1,0:T(8,128)(2,1)} %bitcast.478), kind=kOutput, calls=%fused_computation.96 | convolution fusion | flops 7085424640 | bytes 37552128 | tf_op jit(solution)/shard_map/dot_general | solution.py:61
  381.1 11.4 %fusion.156 = f32[1024,1536]{1,0:T(8,128)S(1)} fusion(bf16[1024,2240]{0,1:T(8,128)(2,1)} %get-tuple-element.81, bf16[1536,2240]{1,0:T(8,128)(2,1)} %bitcast.483), kind=kOutput, calls=%fused_computation.346 | convolution fusion | flops 7046430720 | bytes 17760256 | tf_op jit(solution)/shard_map/dot_general | solution.py:61
  392.5 11.9 %convolution_add_fusion.1 = f32[1024,1536]{1,0:T(8,128)} fusion(f32[1024,1536]{1,0:T(8,128)S(1)} %fusion.156, bf16[1024,2240]{0,1:T(8,128)(2,1)S(1)} %copy-done.102, bf16[1536,2240]{1,0:T(8,128)(2,1)} %bitcast.479), kind=kOutput, calls=%fused_computation.139 | convolution fusion | flops 7048003584 | bytes 24051712 | tf_op jit(solution)/shard_map/dot_general | solution.py:61
  405.2 4.4 sort.15
  410.9 11.5 %fusion.155 = f32[1024,1536]{1,0:T(8,128)S(1)} fusion(bf16[1024,2240]{0,1:T(8,128)(2,1)} %get-tuple-element.77, bf16[2240,1536]{1,0:T(8,128)(2,1)} %bitcast.485), kind=kOutput, calls=%fused_computation.345 | convolution fusion | flops 7046430720 | bytes 17760256 | tf_op jit(solution)/shard_map/dot_general | solution.py:61
  431.0 20.1 %fusion.43 = f32[1536,2240]{1,0:T(8,128)S(1)} fusion(bf16[2048,1536]{1,0:T(8,128)(2,1)S(1)} %constant_dynamic-update-slice_fusion.20, bf16[1024,2240]{0,1:T(8,128)(2,1)} %get-tuple-element.83, bf16[1024,2240]{0,1:T(8,128)(2,1)} %get-tuple-element.81), kind=kOutput, calls=%fused_computation.104 | convolution fusion | flops 14111211520 | bytes 29229056 | tf_op jit(solution)/shard_map/dot_general | solution.py:61
  451.1 3.9 dynamic-slice_bitcast_fusion.15
  454.9 5.9 copy-done.11
  461.1 21.3 %fusion.39 = f32[1536,2240]{1,0:T(8,128)S(1)} fusion(bf16[2048,1536]{1,0:T(8,128)(2,1)} %copy-done.41, bf16[1024,2240]{0,1:T(8,128)(2,1)} %get-tuple-element.82, bf16[1024,2240]{0,1:T(8,128)(2,1)} %get-tuple-element.80), kind=kOutput, calls=%fused_computation.100 | convolution fusion | flops 14111211520 | bytes 29229056 | tf_op jit(solution)/shard_map/dot_general | solution.py:61
  482.5 3.7 dynamic-slice_bitcast_fusion.16
  489.8 4.0 pad_maximum_fusion
  502.8 5.0 convolution_convert_fusion.4
  508.6 8.1 fusion.29
  516.8 11.2 %fusion.109 = f32[1,512,2,128]{3,1,2,0:T(8,128)S(1)} fusion(bf16[2,6,512,512]{2,3,1,0:T(8,128)(2,1)S(1)} %get-tuple-element.231, f32[2,6,512]{2,1,0:T(8,128)S(1)} %neg.22, f32[2,6,512]{2,1,0:T(8,128)S(1)} %copy-done.75, pred[512,512]{0,1:T(8,128)(4,1)S(1)} %copy-done.38, f32[2,512,512,6]{2,1,3,0:T(8,128)} %copy-done.2, f32[2,6,512]{2,1,0:T(8,128)S(1)} %copy-done.71, ...), kind=kOutput, calls=%fused_computation.224 | convolution fusion | flops 837025792 | bytes 21307392 | tf_op jit(solution)/shard_map/transpose(jvp(bqkgd,bskd->bkgqs))/dot_general | solution.py:47
  529.4 4.6 fusion.84
  538.0 9.3 bitcast_convert_fusion
  551.3 5.9 fusion.97
  557.2 5.2 fusion.113
  568.8 5.4 bitcast_add_fusion.5
  574.3 18.8 %fusion.158 = f32[2,2,560,1536]{3,2,1,0:T(8,128)S(1)} fusion(bf16[2,2,560,2048]{3,2,1,0:T(8,128)(2,1)} %bitcast.475, bf16[2048,1536,1,1]{1,0,3,2:T(8,128)(2,1)} %bitcast.149), kind=kOutput, calls=%fused_computation.348 | convolution fusion | flops 14092861440 | bytes 29229056 | tf_op jit(solution)/shard_map/dot_general | solution.py:61
  593.1 3.8 dynamic-slice_bitcast_fusion.17
  600.7 11.7 %fusion.153 = f32[1024,1536]{1,0:T(8,128)S(1)} fusion(bf16[1024,2240]{0,1:T(8,128)(2,1)} %get-tuple-element.76, bf16[2240,1536]{1,0:T(8,128)(2,1)} %bitcast.486), kind=kOutput, calls=%fused_computation.343 | convolution fusion | flops 7046430720 | bytes 17760256 | tf_op jit(solution)/shard_map/dot_general | solution.py:61
  618.8 6.2 bitcast_add_fusion.1
  630.4 6.2 bitcast_add_fusion.2
  641.3 9.1 bitcast_add_fusion.4
  650.4 5.2 dynamic-slice_bitcast_fusion.28
  667.4 6.6 bitcast_add_fusion.3
  678.8 29.9 %collective-permute-done.52 = f32[4,96,2240]{2,1,0:T(8,128)} collective-permute-done((f32[4,96,2240]{2,1,0:T(8,128)}, f32[4,96,2240]{2,1,0:T(8,128)}, u32[]{:S(2)}, u32[]{:S(2)}) %collective-permute-start.52) | collective-permute-done | bytes 3440672 | tf_op jit(solution)/shard_map/ppermute | solution.py:65
  711.7 71.6 %collective-permute-done.50 = f32[4,96,2240]{2,1,0:T(8,128)} collective-permute-done((f32[4,96,2240]{2,1,0:T(8,128)}, f32[4,96,2240]{2,1,0:T(8,128)}, u32[]{:S(2)}, u32[]{:S(2)}) %collective-permute-start.50) | collective-permute-done | bytes 3440672 | tf_op jit(solution)/shard_map/ppermute | solution.py:65
  789.6 5.2 all-to-all-start.3
  794.8 7.4 fusion.67
  807.7 26.4 %all-to-all-done.3 = bf16[4,2,96,2240]{3,2,1,0:T(8,128)(2,1)} async-done(((bf16[4,2,96,2240]{3,2,1,0:T(8,128)(2,1)}), bf16[4,2,96,2240]{3,2,1,0:T(8,128)(2,1)}, u32[]{:S(2)}, u32[]{:S(2)}) %all-to-all-start.3) | async-done | bytes 3440672 | tf_op jit(solution)/shard_map/all_to_all | solution.py:343
  847.5 54.3 %collective-permute-done.40 = f32[256,768]{1,0:T(8,128)S(1)} collective-permute-done((f32[256,768]{1,0:T(8,128)S(1)}, f32[256,768]{1,0:T(8,128)S(1)}, u32[]{:S(2)}, u32[]{:S(2)}) %collective-permute-start.40) | collective-permute-done | bytes 786464 | tf_op jit(solution)/shard_map/ppermute | solution.py:65
  901.8 8.9 collective-permute-done.38
  914.8 3.8 fusion.63
  923.4 4.1 squeeze.232
  930.1 4.2 squeeze.231
  934.4 21.9 %conditional.3 = (bf16[9496,1536]{1,0:T(8,128)(2,1)}) conditional(s32[]{:T(128)} %convert_element_type.238, (s32[20,768]{1,0:T(8,128)S(1)}, f32[16,48,1536]{2,1,0:T(8,128)}, s32[768]{0:T(1024)S(1)}, s32[768]{0:T(1024)S(1)}) %tuple.129, (s32[]{:T(128)}, s32[16,512]{1,0:T(8,128)S(1)}, s32[16,512]{1,0:T(8,128)S(1)}, ...), branch_computations={%region_23.25_spmd, %region_25.27_spmd} | conditional | flops 40000016384 | bytes 366523680 | solution.py:374
  935.0 19.6 %branch_0_fun.1 = bf16[9496,1536]{1,0:T(8,128)(2,1)} custom-call(s32[20]{0:T(128)} %reduce_sum.90.start_ref, s32[768]{0:T(1024)S(1)} %get-tuple-element.44.slot_ref, s32[768]{0:T(1024)S(1)} %get-tuple-element.45.row_ref, f32[768,1536]{1,0:T(8,128)} %bitcast.17.recv_ref), custom_call_target="tpu_custom_call" | custom-call | flops 40000000000 | bytes 40000000 | tf_op jit(solution)/shard_map/cond/branch_0_fun/pallas_call | solution.py:88
  962.7 10.9 %collective-permute-done.48 = f32[96,1536]{1,0:T(8,128)S(1)} collective-permute-done((f32[96,1536]{1,0:T(8,128)S(1)}, f32[96,1536]{1,0:T(8,128)S(1)}, u32[]{:S(2)}, u32[]{:S(2)}) %collective-permute-start.48) | collective-permute-done | bytes 589856 | tf_op jit(solution)/shard_map/ppermute | solution.py:65
  975.5 12.9 %collective-permute-done.46 = f32[96,2048]{1,0:T(8,128)S(1)} collective-permute-done((f32[96,2048]{1,0:T(8,128)S(1)}, f32[96,2048]{1,0:T(8,128)S(1)}, u32[]{:S(2)}, u32[]{:S(2)}) %collective-permute-start.46) | collective-permute-done | bytes 786464 | tf_op jit(solution)/shard_map/ppermute | solution.py:65
  (430 shorter events, 215.5 us)
Async XLA Ops:
  7.2 110.4 %all-gather.5.cloned.1.call-start = ((), (), s32[]{:S(2)}) async-start(), calls=%async_computation.8 | async-start | bytes 6684672 | tf_op jit(solution)/shard_map/all_gather | solution.py:263
  9.8 145.8 %all-gather.7.cloned.1.call-start = ((), (), s32[]{:S(2)}) async-start(), calls=%async_computation.9 | async-start | bytes 5013504 | tf_op jit(solution)/shard_map/all_gather | solution.py:264
  26.3 71.9 %copy-start.61 = (s32[16,512]{1,0:T(8,128)}, s32[16,512]{1,0:T(8,128)S(1)}, u32[]{:S(2)}) copy-start(s32[16,512]{1,0:T(8,128)S(1)} %broadcast_subtract_fusion) | copy-start | bytes 98308
  30.6 67.6 %copy-start.65 = (s32[16,512]{1,0:T(8,128)}, s32[16,512]{1,0:T(8,128)S(1)}, u32[]{:S(2)}) copy-start(s32[16,512]{1,0:T(8,128)S(1)} %get-tuple-element.165) | copy-start | bytes 98308
  32.9 20.7 %copy-start.88 = (pred[16,48]{1,0:T(8,128)(4,1)}, pred[16,48]{1,0:T(8,128)(4,1)S(1)}, u32[]{:S(2)}) copy-start(pred[16,48]{1,0:T(8,128)(4,1)S(1)} %fusion.88) | copy-start | bytes 2308
  33.3 20.2 %copy-start.77 = (s32[16,48]{1,0:T(8,128)}, s32[16,48]{1,0:T(8,128)S(1)}, u32[]{:S(2)}) copy-start(s32[16,48]{1,0:T(8,128)S(1)} %select_reduce_fusion) | copy-start | bytes 9220
  53.5 41.1 %copy-start.76 = (s32[1,512]{1,0:T(1,128)S(1)}, s32[1,512]{1,0:T(1,128)}, u32[]{:S(2)}) copy-start(s32[1,512]{1,0:T(1,128)} %param.20) | copy-start | bytes 6148
  103.6 14.0 %copy-start.13 = (f32[512,1536]{1,0:T(8,128)}, f32[512,1536]{1,0:T(8,128)S(1)}, u32[]{:S(2)}) copy-start(f32[512,1536]{1,0:T(8,128)S(1)} %get-tuple-element.74) | copy-start | bytes 9437188
  103.6 67.3 %collective-permute-start.33 = (bf16[512,1536]{1,0:T(8,128)(2,1)}, bf16[512,1536]{1,0:T(8,128)(2,1)}, u32[]{:S(2)}, u32[]{:S(2)}) collective-permute-start(bf16[512,1536]{1,0:T(8,128)(2,1)} %bitcast.495), channel_id=1, source_target_pairs={{0,4},{4,0},{1,5},{5,1},{2,6},{6,2},{3,7},{7,3},{8,12},{12,8},{9,1... | collective-permute-start | bytes 4718600 | tf_op jit(solution)/shard_map/ppermute | solution.py:65
  105.2 69.0 %collective-permute-start.32 = (bf16[512,1536]{1,0:T(8,128)(2,1)}, bf16[512,1536]{1,0:T(8,128)(2,1)}, u32[]{:S(2)}, u32[]{:S(2)}) collective-permute-start(bf16[512,1536]{1,0:T(8,128)(2,1)} %bitcast.496), channel_id=1, source_target_pairs={{0,8},{8,0},{1,9},{9,1},{2,10},{10,2},{3,11},{11,3},{4,12},{12,4},... | collective-permute-start | bytes 4718600 | tf_op jit(solution)/shard_map/ppermute | solution.py:65
  105.8 100.9 %collective-permute-start.36 = (bf16[1,560,1536]{2,1,0:T(8,128)(2,1)}, bf16[1,560,1536]{2,1,0:T(8,128)(2,1)}, u32[]{:S(2)}, u32[]{:S(2)}) collective-permute-start(bf16[1,560,1536]{2,1,0:T(8,128)(2,1)} %bitcast.507), channel_id=1, source_target_pairs={{0,2},{2,0},{1,3},{3,1},{4,6},{6,4},{5,7},{7,5},{8,10},{10,8},{9,1... | collective-permute-start | bytes 5160968 | tf_op jit(solution)/shard_map/ppermute | solution.py:65
  109.1 54.9 %all-to-all-start.1 = ((bf16[4,96,2240]{2,1,0:T(8,128)(2,1)}), bf16[4,96,2240]{2,1,0:T(8,128)(2,1)}, u32[]{:S(2)}, u32[]{:S(2)}) async-start(bf16[4,96,2240]{2,1,0:T(8,128)(2,1)} %pad_maximum_fusion.4), calls=%async_computation.1 | async-start | bytes 3538944 | tf_op jit(solution)/shard_map/all_to_all | solution.py:275
  114.1 47.2 %copy-start.72 = (f32[1536]{0:T(1024)}, f32[1536]{0:T(1024)S(1)}, u32[]{:S(2)}) copy-start(f32[1536]{0:T(1024)S(1)} %mul.383) | copy-start | bytes 18436
  114.2 33.3 %copy-start.37 = (pred[512,512]{0,1:T(8,128)(4,1)}, pred[512,512]{0,1:T(8,128)(4,1)S(1)}, u32[]{:S(2)}) copy-start(pred[512,512]{0,1:T(8,128)(4,1)S(1)} %iota_compare_fusion.4) | copy-start | bytes 786436
  164.0 35.4 %all-to-all-start = ((bf16[4,96,2240]{2,1,0:T(8,128)(2,1)}), bf16[4,96,2240]{2,1,0:T(8,128)(2,1)S(1)}, u32[]{:S(2)}, u32[]{:S(2)}) async-start(bf16[4,96,2240]{2,1,0:T(8,128)(2,1)} %pad_maximum_fusion.3), calls=%async_computation | async-start | bytes 3538944 | tf_op jit(solution)/shard_map/all_to_all | solution.py:275
  168.2 107.6 %all-gather.11.cloned.1.call-start = ((), (), s32[]{:S(2)}) async-start(), calls=%async_computation.11 | async-start | bytes 3932160 | tf_op jit(solution)/shard_map/all_gather | solution.py:307
  170.9 174.4 %all-gather.9.cloned.1.call-start = ((), (), s32[]{:S(2)}) async-start(), calls=%async_computation.10 | async-start | bytes 3932160 | tf_op jit(solution)/shard_map/all_gather | solution.py:307
  172.1 45.3 %collective-permute-start.35 = (bf16[512,768]{1,0:T(8,128)(2,1)S(1)}, bf16[512,768]{1,0:T(8,128)(2,1)}, u32[]{:S(2)}, u32[]{:S(2)}) collective-permute-start(bf16[512,768]{1,0:T(8,128)(2,1)S(1)} %slice.185), channel_id=1, source_target_pairs={{0,8},{8,0},{1,9},{9,1},{2,10},{10,2},{3,11},{11,3},{4,12},{12,4},... | collective-permute-start | bytes 2359304 | tf_op jit(solution)/shard_map/ppermute | solution.py:65
  176.3 42.3 %collective-permute-start.34 = (bf16[512,768]{1,0:T(8,128)(2,1)}, bf16[512,768]{1,0:T(8,128)(2,1)}, u32[]{:S(2)}, u32[]{:S(2)}) collective-permute-start(bf16[512,768]{1,0:T(8,128)(2,1)} %slice.184), channel_id=1, source_target_pairs={{0,4},{4,0},{1,5},{5,1},{2,6},{6,2},{3,7},{7,3},{8,12},{12,8},{9,1... | collective-permute-start | bytes 2359304 | tf_op jit(solution)/shard_map/ppermute | solution.py:65
  182.1 85.2 %collective-permute-start.31 = (bf16[4,96,2240]{2,1,0:T(8,128)(2,1)}, bf16[4,96,2240]{2,1,0:T(8,128)(2,1)}, u32[]{:S(2)}, u32[]{:S(2)}) collective-permute-start(bf16[4,96,2240]{2,1,0:T(8,128)(2,1)} %all-to-all-done.1.own_ref), channel_id=1, source_target_pairs={{0,2},{2,0},{1,3},{3,1},{4,6},{6,4},{5,7},{7,5},{8,10},{10,8},{9,1... | collective-permute-start | bytes 5160968 | tf_op jit(solution)/shard_map/ppermute | solution.py:65
  199.4 15.6 %copy-start.22 = (bf16[4,96,2240]{2,1,0:T(8,128)(2,1)}, bf16[4,96,2240]{2,1,0:T(8,128)(2,1)S(1)}, u32[]{:S(2)}) copy-start(bf16[4,96,2240]{2,1,0:T(8,128)(2,1)S(1)} %all-to-all-done.own_ref) | copy-start | bytes 5160964
  199.4 59.5 %collective-permute-start.30 = (bf16[4,96,2240]{2,1,0:T(8,128)(2,1)S(1)}, bf16[4,96,2240]{2,1,0:T(8,128)(2,1)}, u32[]{:S(2)}, u32[]{:S(2)}) collective-permute-start(bf16[4,96,2240]{2,1,0:T(8,128)(2,1)S(1)} %all-to-all-done.own_ref), channel_id=1, source_target_pairs={{0,2},{2,0},{1,3},{3,1},{4,6},{6,4},{5,7},{7,5},{8,10},{10,8},{9,1... | collective-permute-start | bytes 5160968 | tf_op jit(solution)/shard_map/ppermute | solution.py:65
  275.7 218.1 %reduce-scatter.7.cloned.1.call-start = ((), (), s32[]{:S(2)}) async-start(), calls=%async_computation.13 | async-start | bytes 7864320 | tf_op jit(solution)/shard_map/reduce_scatter | solution.py:315
  275.8 13.6 %copy-start.39 = (bf16[1024,1536]{1,0:T(8,128)(2,1)S(1)}, bf16[1024,1536]{1,0:T(8,128)(2,1)}, u32[]{:S(2)}) copy-start(bf16[1024,1536]{1,0:T(8,128)(2,1)} %all-gather.11.cloned.1.call-done) | copy-start | bytes 9437188
  309.7 11.9 %copy-start.101 = (bf16[1024,2240]{0,1:T(8,128)(2,1)S(1)}, bf16[1024,2240]{0,1:T(8,128)(2,1)}, u32[]{:S(2)}) copy-start(bf16[1024,2240]{0,1:T(8,128)(2,1)} %get-tuple-element.82) | copy-start | bytes 13762564
  333.4 163.9 %reduce-scatter.5.cloned.1.call-start = ((), (), s32[]{:S(2)}) async-start(), calls=%async_computation.12 | async-start | bytes 7864320 | tf_op jit(solution)/shard_map/reduce_scatter | solution.py:315
  381.1 11.4 %copy-start.102 = (bf16[1024,2240]{0,1:T(8,128)(2,1)S(1)}, bf16[1024,2240]{0,1:T(8,128)(2,1)}, u32[]{:S(2)}) copy-start(bf16[1024,2240]{0,1:T(8,128)(2,1)} %get-tuple-element.80) | copy-start | bytes 13762564
  404.4 551.8 %reduce-scatter.11.cloned.1.call-start = ((), (), s32[]{:S(2)}) async-start(), calls=%async_computation.15 | async-start | bytes 5898240 | tf_op jit(solution)/shard_map/reduce_scatter | solution.py:336
  429.2 227.7 %collective-permute-start.43 = (f32[2,256,768]{2,1,0:T(8,128)}, f32[2,256,768]{2,1,0:T(8,128)}, u32[]{:S(2)}, u32[]{:S(2)}) collective-permute-start(f32[2,256,768]{2,1,0:T(8,128)} %slice.196), channel_id=1, source_target_pairs={{0,4},{4,0},{1,5},{5,1},{2,6},{6,2},{3,7},{7,3},{8,12},{12,8},{9,1... | collective-permute-start | bytes 4718600 | tf_op jit(solution)/shard_map/ppermute | solution.py:65
  430.9 20.1 %copy-start.41 = (bf16[2048,1536]{1,0:T(8,128)(2,1)}, bf16[2048,1536]{1,0:T(8,128)(2,1)S(1)}, u32[]{:S(2)}) copy-start(bf16[2048,1536]{1,0:T(8,128)(2,1)S(1)} %constant_dynamic-update-slice_fusion.20) | copy-start | bytes 18874372
  451.0 38.7 %slice-start.11 = ((s8[4587520]{0:T(1024)(128)(4,1)}), s8[4194304]{0:T(1024)(128)(4,1)S(1)}, s32[]{:S(2)}) async-start(s8[4587520]{0:T(1024)(128)(4,1)} %bitcast.499), calls=%async_computation.27 | async-start | bytes 8388608
  451.0 38.7 %slice-start.13 = ((s8[4587520]{0:T(1024)(128)(4,1)}), s8[4194304]{0:T(1024)(128)(4,1)S(1)}, s32[]{:S(2)}) async-start(s8[4587520]{0:T(1024)(128)(4,1)} %bitcast.501), calls=%async_computation.29 | async-start | bytes 8388608
  460.8 28.9 %slice-start.12 = ((s8[4587520]{0:T(1024)(128)(4,1)}), s8[393216]{0:T(1024)(128)(4,1)S(1)}, s32[]{:S(2)}) async-start(s8[4587520]{0:T(1024)(128)(4,1)} %bitcast.499), calls=%async_computation.28 | async-start | bytes 786432
  460.8 28.9 %slice-start.14 = ((s8[4587520]{0:T(1024)(128)(4,1)}), s8[393216]{0:T(1024)(128)(4,1)S(1)}, s32[]{:S(2)}) async-start(s8[4587520]{0:T(1024)(128)(4,1)} %bitcast.501), calls=%async_computation.30 | async-start | bytes 786432
  460.9 156.4 %collective-permute-start.51 = (f32[4,2,96,2240]{3,2,1,0:T(8,128)}, f32[4,2,96,2240]{3,2,1,0:T(8,128)}, u32[]{:S(2)}, u32[]{:S(2)}) collective-permute-start(f32[4,2,96,2240]{3,2,1,0:T(8,128)} %dynamic-slice_bitcast_fusion.15), channel_id=1, source_target_pairs={{0,1},{1,0},{2,3},{3,2},{4,5},{5,4},{6,7},{7,6},{8,9},{9,8},{10,11... | collective-permute-start | bytes 20643848 | tf_op jit(solution)/shard_map/ppermute | solution.py:65
  489.5 139.5 %collective-permute-start.49 = (f32[4,2,96,2240]{3,2,1,0:T(8,128)}, f32[4,2,96,2240]{3,2,1,0:T(8,128)}, u32[]{:S(2)}, u32[]{:S(2)}) collective-permute-start(f32[4,2,96,2240]{3,2,1,0:T(8,128)} %dynamic-slice_bitcast_fusion.16), channel_id=1, source_target_pairs={{0,1},{1,0},{2,3},{3,2},{4,5},{5,4},{6,7},{7,6},{8,9},{9,8},{10,11... | collective-permute-start | bytes 20643848 | tf_op jit(solution)/shard_map/ppermute | solution.py:65
  516.7 11.3 %copy-start.100 = (bf16[2,6,512,512]{2,3,1,0:T(8,128)(2,1)}, bf16[2,6,512,512]{2,3,1,0:T(8,128)(2,1)S(1)}, u32[]{:S(2)}) copy-start(bf16[2,6,512,512]{2,3,1,0:T(8,128)(2,1)S(1)} %get-tuple-element.231) | copy-start | bytes 18874372
  516.7 11.3 %copy-start.80 = (f32[2,6,512]{2,1,0:T(8,128)}, f32[2,6,512]{2,1,0:T(8,128)S(1)}, u32[]{:S(2)}) copy-start(f32[2,6,512]{2,1,0:T(8,128)S(1)} %neg.22) | copy-start | bytes 73732
  516.8 11.3 %copy-start.59 = (f32[512,64]{1,0:T(8,128)S(1)}, f32[512,64]{1,0:T(8,128)}, u32[]{:S(2)}) copy-start(f32[512,64]{1,0:T(8,128)} %constant.390) | copy-start | bytes 393220
  537.0 31.8 %collective-permute-start.47 = (f32[4,2,96,1536]{3,2,1,0:T(8,128)}, f32[4,2,96,1536]{3,2,1,0:T(8,128)}, u32[]{:S(2)}, u32[]{:S(2)}) collective-permute-start(f32[4,2,96,1536]{3,2,1,0:T(8,128)} %dynamic-slice_bitcast_fusion.19), channel_id=1, source_target_pairs={{0,1},{1,0},{2,3},{3,2},{4,5},{5,4},{6,7},{7,6},{8,9},{9,8},{10,11... | collective-permute-start | bytes 14155784 | tf_op jit(solution)/shard_map/ppermute | solution.py:65
  568.8 72.0 %collective-permute-start.45 = (f32[4,2,96,2048]{3,2,1,0:T(8,128)}, f32[4,2,96,2048]{3,2,1,0:T(8,128)}, u32[]{:S(2)}, u32[]{:S(2)}) collective-permute-start(f32[4,2,96,2048]{3,2,1,0:T(8,128)} %dynamic-slice_bitcast_fusion.18), channel_id=1, source_target_pairs={{0,1},{1,0},{2,3},{3,2},{4,5},{5,4},{6,7},{7,6},{8,9},{9,8},{10,11... | collective-permute-start | bytes 18874376 | tf_op jit(solution)/shard_map/ppermute | solution.py:65
  574.3 385.3 %reduce-scatter.9.cloned.1.call-start = ((), (), s32[]{:S(2)}) async-start(), calls=%async_computation.14 | async-start | bytes 7864320 | tf_op jit(solution)/shard_map/reduce_scatter | solution.py:336
  600.1 65.2 %collective-permute-start.53 = (f32[2,560,1536]{2,1,0:T(8,128)}, f32[2,560,1536]{2,1,0:T(8,128)}, u32[]{:S(2)}, u32[]{:S(2)}) collective-permute-start(f32[2,560,1536]{2,1,0:T(8,128)} %dynamic-slice_bitcast_fusion.17), channel_id=1, source_target_pairs={{0,1},{1,0},{2,3},{3,2},{4,5},{5,4},{6,7},{7,6},{8,9},{9,8},{10,11... | collective-permute-start | bytes 20643848 | tf_op jit(solution)/shard_map/ppermute | solution.py:65
  617.3 46.4 %collective-permute-start.41 = (f32[2,256,768]{2,1,0:T(8,128)S(1)}, f32[2,256,768]{2,1,0:T(8,128)S(1)}, u32[]{:S(2)}, u32[]{:S(2)}) collective-permute-start(f32[2,256,768]{2,1,0:T(8,128)S(1)} %copy-done.43), channel_id=1, source_target_pairs={{0,8},{8,0},{1,9},{9,1},{2,10},{10,2},{3,11},{11,3},{4,12},{12,4},... | collective-permute-start | bytes 4718600 | tf_op jit(solution)/shard_map/ppermute | solution.py:65
  629.0 79.7 %collective-permute-start.52 = (f32[4,96,2240]{2,1,0:T(8,128)}, f32[4,96,2240]{2,1,0:T(8,128)}, u32[]{:S(2)}, u32[]{:S(2)}) collective-permute-start(f32[4,96,2240]{2,1,0:T(8,128)} %dynamic-slice_bitcast_fusion.20), channel_id=1, source_target_pairs={{0,2},{2,0},{1,3},{3,1},{4,6},{6,4},{5,7},{7,5},{8,10},{10,8},{9,1... | collective-permute-start | bytes 10321928 | tf_op jit(solution)/shard_map/ppermute | solution.py:65
  640.8 142.6 %collective-permute-start.50 = (f32[4,96,2240]{2,1,0:T(8,128)}, f32[4,96,2240]{2,1,0:T(8,128)}, u32[]{:S(2)}, u32[]{:S(2)}) collective-permute-start(f32[4,96,2240]{2,1,0:T(8,128)} %dynamic-slice_bitcast_fusion.21), channel_id=1, source_target_pairs={{0,2},{2,0},{1,3},{3,1},{4,6},{6,4},{5,7},{7,5},{8,10},{10,8},{9,1... | collective-permute-start | bytes 10321928 | tf_op jit(solution)/shard_map/ppermute | solution.py:65
  656.9 180.8 %collective-permute-start.39 = (f32[2,256,768]{2,1,0:T(8,128)}, f32[2,256,768]{2,1,0:T(8,128)}, u32[]{:S(2)}, u32[]{:S(2)}) collective-permute-start(f32[2,256,768]{2,1,0:T(8,128)} %slice.190), channel_id=1, source_target_pairs={{0,4},{4,0},{1,5},{5,1},{2,6},{6,2},{3,7},{7,3},{8,12},{12,8},{9,1... | collective-permute-start | bytes 4718600 | tf_op jit(solution)/shard_map/ppermute | solution.py:65
  663.7 177.9 %collective-permute-start.37 = (f32[2,256,768]{2,1,0:T(8,128)}, f32[2,256,768]{2,1,0:T(8,128)}, u32[]{:S(2)}, u32[]{:S(2)}) collective-permute-start(f32[2,256,768]{2,1,0:T(8,128)} %slice.188), channel_id=1, source_target_pairs={{0,8},{8,0},{1,9},{9,1},{2,10},{10,2},{3,11},{11,3},{4,12},{12,4},... | collective-permute-start | bytes 4718600 | tf_op jit(solution)/shard_map/ppermute | solution.py:65
  664.4 45.0 %slice-start.3 = ((s8[7077888]{0:T(1024)(128)(4,1)}), s8[4194304]{0:T(1024)(128)(4,1)S(1)}, s32[]{:S(2)}) async-start(s8[7077888]{0:T(1024)(128)(4,1)} %bitcast.455), calls=%async_computation.19 | async-start | bytes 8388608
  665.3 44.0 %slice-start.4 = ((s8[7077888]{0:T(1024)(128)(4,1)}), s8[2883584]{0:T(1024)(128)(4,1)S(1)}, s32[]{:S(2)}) async-start(s8[7077888]{0:T(1024)(128)(4,1)} %bitcast.455), calls=%async_computation.20 | async-start | bytes 5767168
  665.7 179.2 %collective-permute-start.44 = (f32[256,768]{1,0:T(8,128)}, f32[256,768]{1,0:T(8,128)}, u32[]{:S(2)}, u32[]{:S(2)}) collective-permute-start(f32[256,768]{1,0:T(8,128)} %dynamic-slice_bitcast_fusion.32), channel_id=1, source_target_pairs={{0,8},{8,0},{1,9},{9,1},{2,10},{10,2},{3,11},{11,3},{4,12},{12,4},... | collective-permute-start | bytes 2359304 | tf_op jit(solution)/shard_map/ppermute | solution.py:65
  674.0 110.7 %slice-start.5 = ((s8[7077888]{0:T(1024)(128)(4,1)}), s8[4194304]{0:T(1024)(128)(4,1)S(1)}, s32[]{:S(2)}) async-start(s8[7077888]{0:T(1024)(128)(4,1)} %bitcast.457), calls=%async_computation.21 | async-start | bytes 8388608
  678.8 105.9 %slice-start.6 = ((s8[7077888]{0:T(1024)(128)(4,1)}), s8[2883584]{0:T(1024)(128)(4,1)S(1)}, s32[]{:S(2)}) async-start(s8[7077888]{0:T(1024)(128)(4,1)} %bitcast.457), calls=%async_computation.22 | async-start | bytes 5767168
  708.8 137.5 %collective-permute-start.42 = (f32[256,768]{1,0:T(8,128)}, f32[256,768]{1,0:T(8,128)}, u32[]{:S(2)}, u32[]{:S(2)}) collective-permute-start(f32[256,768]{1,0:T(8,128)} %dynamic-slice_bitcast_fusion.33), channel_id=1, source_target_pairs={{0,4},{4,0},{1,5},{5,1},{2,6},{6,2},{3,7},{7,3},{8,12},{12,8},{9,1... | collective-permute-start | bytes 2359304 | tf_op jit(solution)/shard_map/ppermute | solution.py:65
  783.3 130.7 %collective-permute-start.54 = (f32[560,1536]{1,0:T(8,128)}, f32[560,1536]{1,0:T(8,128)}, u32[]{:S(2)}, u32[]{:S(2)}) collective-permute-start(f32[560,1536]{1,0:T(8,128)} %dynamic-slice_bitcast_fusion.22), channel_id=1, source_target_pairs={{0,2},{2,0},{1,3},{3,1},{4,6},{6,4},{5,7},{7,5},{8,10},{10,8},{9,1... | collective-permute-start | bytes 10321928 | tf_op jit(solution)/shard_map/ppermute | solution.py:65
  789.6 44.6 %all-to-all-start.3 = ((bf16[4,2,96,2240]{3,2,1,0:T(8,128)(2,1)}), bf16[4,2,96,2240]{3,2,1,0:T(8,128)(2,1)}, u32[]{:S(2)}, u32[]{:S(2)}) async-start(bf16[4,2,96,2240]{3,2,1,0:T(8,128)(2,1)} %copy.201), calls=%async_computation.7 | async-start | bytes 7077888 | tf_op jit(solution)/shard_map/all_to_all | solution.py:343
  807.7 30.0 %copy-start.21 = (f32[2,256,1536]{2,1,0:T(8,128)S(1)}, f32[2,256,1536]{2,1,0:T(8,128)}, u32[]{:S(2)}) copy-start(f32[2,256,1536]{2,1,0:T(8,128)} %get-tuple-element.189) | copy-start | bytes 9437188
  834.1 100.2 %all-to-all-start.2 = ((f32[16,48,1536]{2,1,0:T(8,128)}), f32[16,48,1536]{2,1,0:T(8,128)}, u32[]{:S(2)}, u32[]{:S(2)}) async-start(f32[16,48,1536]{2,1,0:T(8,128)} %select_select_fusion.1), calls=%async_computation.4 | async-start | bytes 9437184 | tf_op jit(solution)/shard_map/all_to_all | solution.py:360
  839.6 62.2 %collective-permute-start.40 = (f32[256,768]{1,0:T(8,128)S(1)}, f32[256,768]{1,0:T(8,128)S(1)}, u32[]{:S(2)}, u32[]{:S(2)}) collective-permute-start(f32[256,768]{1,0:T(8,128)S(1)} %dynamic-slice_bitcast_fusion.34), channel_id=1, source_target_pairs={{0,8},{8,0},{1,9},{9,1},{2,10},{10,2},{3,11},{11,3},{4,12},{12,4},... | collective-permute-start | bytes 2359304 | tf_op jit(solution)/shard_map/ppermute | solution.py:65
  843.4 67.3 %collective-permute-start.38 = (f32[256,768]{1,0:T(8,128)S(1)}, f32[256,768]{1,0:T(8,128)S(1)}, u32[]{:S(2)}, u32[]{:S(2)}) collective-permute-start(f32[256,768]{1,0:T(8,128)S(1)} %dynamic-slice_bitcast_fusion.35), channel_id=1, source_target_pairs={{0,4},{4,0},{1,5},{5,1},{2,6},{6,2},{3,7},{7,3},{8,12},{12,8},{9,1... | collective-permute-start | bytes 2359304 | tf_op jit(solution)/shard_map/ppermute | solution.py:65
  956.3 34.3 %copy-start.1 = (bf16[96,12,128]{2,0,1:T(8,128)(2,1)S(1)}, bf16[96,12,128]{2,0,1:T(8,128)(2,1)}, u32[]{:S(2)}) copy-start(bf16[96,12,128]{2,0,1:T(8,128)(2,1)} %param.25) | copy-start | bytes 884740
  957.5 16.2 %collective-permute-start.48 = (f32[96,1536]{1,0:T(8,128)S(1)}, f32[96,1536]{1,0:T(8,128)S(1)}, u32[]{:S(2)}, u32[]{:S(2)}) collective-permute-start(f32[96,1536]{1,0:T(8,128)S(1)} %dynamic-slice_bitcast_fusion.36), channel_id=1, source_target_pairs={{0,2},{2,0},{1,3},{3,1},{4,6},{6,4},{5,7},{7,5},{8,10},{10,8},{9,1... | collective-permute-start | bytes 1769480 | tf_op jit(solution)/shard_map/ppermute | solution.py:65
  959.6 28.8 %copy-start.42 = (f32[192,2048]{1,0:T(8,128)S(1)}, f32[192,2048]{1,0:T(8,128)}, u32[]{:S(2)}) copy-start(f32[192,2048]{1,0:T(8,128)} %reduce-scatter.9.cloned.1.call-done) | copy-start | bytes 4718596
  960.9 27.5 %collective-permute-start.46 = (f32[96,2048]{1,0:T(8,128)S(1)}, f32[96,2048]{1,0:T(8,128)S(1)}, u32[]{:S(2)}, u32[]{:S(2)}) collective-permute-start(f32[96,2048]{1,0:T(8,128)S(1)} %dynamic-slice_bitcast_fusion.31), channel_id=1, source_target_pairs={{0,2},{2,0},{1,3},{3,1},{4,6},{6,4},{5,7},{7,5},{8,10},{10,8},{9,1... | collective-permute-start | bytes 2359304 | tf_op jit(solution)/shard_map/ppermute | solution.py:65
  (81 other events, 420.9 us)
Sparse Core Ops, SparseCore 0:
  10.2 45.6 all-gather.4
  58.1 54.9 all-gather.6
  171.4 59.8 all-gather.10
  275.9 39.4 all-gather.8
  333.5 65.6 reduce-scatter.6
  404.6 92.6 reduce-scatter.4
  574.4 59.7 reduce-scatter.10
  650.6 112.2 reduce-scatter.8
